TPU v7x, 256 devices: a whole 4x4x8 slice. The times are simulated.
256 devices in a mesh: gx: 32 (over x, y, core), gy: 8 (over z).
Axes of the slice: x: 4, y: 4, z: 8, core: 2. Of those that a mesh axis runs over, the one named last changes fastest.
Arguments:
- rhs_conc: float32 [64, 128, 2048], P('gx', 'gy'), may hold values from -60 to 60
- rhs_pots: float32 [64, 128, 33], P('gx', 'gy'), may hold values from -60 to 60
- diffusion: float32 [64, 128, 32], P('gx', 'gy'), may hold values from 0.05 to 5
- exchange: float32 [64, 128, 32], P('gx', 'gy'), may hold values from 0.2 to 4
- slope: float32 [64, 128, 32], P('gx', 'gy'), may hold values from 0.1 to 1
Outputs:
- sol_conc: float32 [64, 128, 2048], P('gx', 'gy')
- sol_pots: float32 [64, 128, 33], P('gx', 'gy')
All inputs are finite; a program needn't handle non-finite values.
Results may differ from a plain program's by a relative error of at most 0.0003.
Values sent between devices are 32-bit elements; how exact they have to be, the bound alone decides.
A program may use at most 64 MiB of HBM per device.

v0:
```python
import functools
import jax
import jax.numpy as jnp
from jax import lax
from jax.experimental import pallas as pl
from jax.experimental.pallas import tpu as pltpu
from jax.sharding import Mesh
from jax.sharding import PartitionSpec as P

ITERS = 10
MESH = pl.DeviceIdType.MESH
GX = ("gx_0", "gx_1", "gx_2")

node_cond = 1.0
plane_cond = 0.5
collector_cond = 2.0
epsilon = 1e-06

CENTER = 11.0
HALF = 10.0
TRUST = 1e-4

CELLS = 32
SHELLS = 64
DIM = ITERS + 1


def kernel(nx, ny, conc, pots, diff, exch, slope, out_c, out_p, flag,
           tall, vecs, planes, halo, rows, sums_a, sums_b,
           hs_sem, hr_sem, as_sem, ar_sem, bs_sem, br_sem):
    n_a = nx // 2
    n_b = 2 * ny
    gx = lax.axis_index("gx")
    gy = lax.axis_index("gy")
    core = lax.rem(gx, 2)
    col = lax.div(gx, 2)
    slot_a = col
    slot_b = core * ny + gy

    def peer_a(step):
        other = lax.rem(col + step, n_a)
        return other, (other * 2 + core, gy)

    def peer_b(step):
        other = lax.rem(slot_b + step, n_b)
        return other, (col * 2 + lax.div(other, ny), lax.rem(other, ny))

    sends = (
        (gx < nx - 1, (gx + 1, gy)),
        (gx > 0, (gx - 1, gy)),
        (gy < ny - 1, (gx, gy + 1)),
        (gy > 0, (gx, gy - 1)),
    )
    receives = (gx > 0, gx < nx - 1, gy > 0, gy < ny - 1)

    barrier = pltpu.get_barrier_semaphore()
    for exists, device in sends:
        @pl.when(exists)
        def _(device=device):
            pl.semaphore_signal(barrier, inc=1, device_id=device, device_id_type=MESH)
    for step in range(1, n_a):
        pl.semaphore_signal(barrier, inc=1, device_id=peer_a(step)[1], device_id_type=MESH)
    for step in range(1, n_b):
        pl.semaphore_signal(barrier, inc=1, device_id=peer_b(step)[1], device_id_type=MESH)

    lane = lax.broadcasted_iota(jnp.int32, (8, 128), 1)
    sub = lax.broadcasted_iota(jnp.int32, (8, 128), 0)
    quarter = lane // 32
    x_of = (lane // 16) % 2
    y_of = lane % 16
    once = jnp.logical_and(sub == 0, quarter == 0)
    zero = jnp.zeros((8, 128), jnp.float32)

    for d in range(4):
        @pl.when(jnp.logical_not(receives[d]))
        def _(d=d):
            for k in range(ITERS):
                halo[k, d] = jnp.zeros((16, 128), jnp.float32)

    def spread(by_node):
        parts = [by_node[8 * q:8 * q + 8, :] for q in range(4)]
        return jnp.concatenate(parts, axis=1)

    def small(ref):
        return spread(ref[...].reshape(CELLS, CELLS).T)

    diffusion = small(diff)
    exchange = small(exch)
    slopes = small(slope)
    pots_t = pots[...].reshape(CELLS, CELLS + 1).T
    pot = spread(pots_t[:CELLS])
    collector = jnp.broadcast_to(
        jnp.concatenate([pots_t[CELLS:CELLS + 1]] * 4, axis=1), (8, 128))
    planes[0, 0:8] = pot
    planes[0, 8:16] = collector
    rows[...] = jnp.zeros((128, 128), jnp.float32)

    flat = conc[...].reshape(CELLS, 2048)
    for g in range(4):
        block = jnp.concatenate(
            [flat[:, (4 * q + g) * 128:(4 * q + g + 1) * 128] for q in range(4)], axis=0)
        tall[g * 128:(g + 1) * 128, :] = block.T

    def first(b, acc):
        for i in range(8):
            r = b * 8 + i
            shell = tall[pl.ds(r, 8, stride=SHELLS), :]
            vecs[0, r] = shell
            acc = acc + shell * shell
        return acc

    def keep(k, i, acc):
        total = jnp.sum(acc, axis=0, keepdims=True)
        rows[DIM * k + i:DIM * k + i + 1, :] = total
        if i != k:
            rows[DIM * i + k:DIM * i + k + 1, :] = total

    acc = lax.fori_loop(0, 8, first, zero)
    keep(0, 0, acc + pot * pot + jnp.where(once, collector * collector, 0.0))

    pl.semaphore_wait(barrier, n_a + n_b - 2 + sum(r.astype(jnp.int32) for r in receives))

    def halo_copy(k, d):
        return pltpu.make_async_remote_copy(
            src_ref=planes.at[k],
            dst_ref=halo.at[k, d],
            send_sem=hs_sem.at[k, d],
            recv_sem=hr_sem.at[k, d],
            device_id=sends[d][1],
            device_id_type=MESH,
        )

    def send_halo(k):
        for d in range(4):
            @pl.when(sends[d][0])
            def _(d=d):
                halo_copy(k, d).start()

    send_halo(0)

    def lateral_inside(v):
        return (4.0 * v
                - jnp.where(x_of == 1, pltpu.roll(v, 16, 1), pltpu.roll(v, 112, 1))
                - jnp.where(y_of > 0, pltpu.roll(v, 1, 1), 0.0)
                - jnp.where(y_of < 15, pltpu.roll(v, 127, 1), 0.0))

    def lateral_outside(k, at):
        low_x, high_x, low_y, high_y = (halo[k, d, at:at + 8] for d in range(4))
        return (jnp.where(x_of == 0, pltpu.roll(low_x, 112, 1), pltpu.roll(high_x, 16, 1))
                + jnp.where(y_of == 0, pltpu.roll(low_y, 113, 1), 0.0)
                + jnp.where(y_of == 15, pltpu.roll(high_y, 15, 1), 0.0))

    def node_mirror(v):
        down = pltpu.roll(v, 1, 0)
        down = jnp.where(sub == 0, pltpu.roll(down, 32, 1), down)
        down = jnp.where(jnp.logical_and(sub == 0, quarter == 0), v, down)
        up = pltpu.roll(v, 7, 0)
        up = jnp.where(sub == 7, pltpu.roll(up, 96, 1), up)
        up = jnp.where(jnp.logical_and(sub == 7, quarter == 3), v, up)
        return 2.0 * v - down - up

    def over_nodes(v):
        v = jnp.broadcast_to(jnp.sum(v, axis=0, keepdims=True), (8, 128))
        v = v + pltpu.roll(v, 64, 1)
        return v + pltpu.roll(v, 32, 1)

    for k in range(ITERS):
        scale = (1.0 if k == 0 else 2.0) / HALF
        pot = planes[k, 0:8]
        collector = planes[k, 8:16]
        current = exchange * (pot - collector)
        own_pot = scale * (
            node_cond * node_mirror(pot) + current - slopes * vecs[k, SHELLS - 1]
            + plane_cond * lateral_inside(pot) - CENTER * pot)
        own_collector = scale * (
            collector_cond * lateral_inside(collector) - over_nodes(current) * (1.0 / 32.0)
            - CENTER * collector)
        if k > 0:
            own_pot = own_pot - planes[k - 1, 0:8]
            own_collector = own_collector - planes[k - 1, 8:16]
        center_coef = scale * (1.0 - CENTER + 2.0 * diffusion)
        side_coef = scale * diffusion

        def shells(base, accs, last, k=k, center_coef=center_coef, side_coef=side_coef,
                   scale=scale, current=current):
            accs = list(accs)
            low = vecs[k, jnp.maximum(base - 1, 0)]
            here = vecs[k, base]
            for i in range(8):
                r = base + i
                high = here if last and i == 7 else vecs[k, r + 1]
                new = center_coef * here - side_coef * (low + high)
                if last and i == 7:
                    new = new + scale * current
                if k > 0:
                    new = new - vecs[k - 1, r]
                vecs[k + 1, r] = new
                for m in range(k):
                    accs[m] = accs[m] + new * vecs[m, r]
                accs[k] = accs[k] + new * here
                accs[k + 1] = accs[k + 1] + new * new
                low, here = here, high
            return tuple(accs)

        accs = lax.fori_loop(
            0, 7, lambda b, accs: shells(b * 8, accs, False), (zero,) * (k + 2))
        accs = shells(SHELLS - 8, accs, True)

        for d in range(4):
            @pl.when(receives[d])
            def _(d=d):
                halo_copy(k, d).wait_recv()
        new_pot = own_pot - (scale * plane_cond) * lateral_outside(k, 0)
        new_collector = own_collector - (scale * collector_cond) * lateral_outside(k, 8)
        planes[k + 1, 0:8] = new_pot
        planes[k + 1, 8:16] = new_collector
        if k + 1 < ITERS:
            send_halo(k + 1)
        for m in range(k + 2):
            acc = accs[m] + new_pot * planes[m, 0:8] + jnp.where(
                once, new_collector * planes[m, 8:16], 0.0)
            keep(k + 1, m, acc)

    def total(mine, count, slot, peer, sums, s_sem, r_sem):
        sums[pl.ds(slot, 1)] = mine.reshape(1, 1, 128)

        def copy(step):
            other, device = peer(step)
            return other, pltpu.make_async_remote_copy(
                src_ref=sums.at[slot],
                dst_ref=sums.at[slot],
                send_sem=s_sem.at[step],
                recv_sem=r_sem.at[slot],
                device_id=device,
                device_id_type=MESH,
            )

        for step in range(1, count):
            copy(step)[1].start()
        for step in range(1, count):
            other = peer(step)[0]
            pltpu.make_async_remote_copy(
                src_ref=sums.at[other],
                dst_ref=sums.at[other],
                send_sem=s_sem.at[step],
                recv_sem=r_sem.at[other],
                device_id=peer(step)[1],
                device_id_type=MESH,
            ).wait_recv()
        return jnp.sum(sums[...], axis=0), copy

    mine = jnp.sum(rows[...].T, axis=0, keepdims=True)
    part, copy_a = total(mine, n_a, slot_a, peer_a, sums_a, as_sem, ar_sem)
    whole, copy_b = total(part, n_b, slot_b, peer_b, sums_b, bs_sem, br_sem)

    lane2 = lax.broadcasted_iota(jnp.int32, (16, 128), 1)
    sub2 = lax.broadcasted_iota(jnp.int32, (16, 128), 0)
    eye = sub2 == lane2
    whole = jnp.broadcast_to(whole, (16, 128))
    gram = jnp.zeros((16, 128), jnp.float32)
    for k in range(DIM):
        moved = whole if k == 0 else pltpu.roll(whole, (128 - DIM * k) % 128, 1)
        gram = jnp.where(sub2 == k, moved, gram)
    gram = jnp.where(lane2 < DIM, gram, 0.0)

    def down(v):
        return jnp.broadcast_to(jnp.sum(v, axis=0, keepdims=True), (16, 128))

    def turned(v):
        return jnp.broadcast_to(
            jnp.sum(jnp.where(eye, v, 0.0), axis=1, keepdims=True), (16, 128))

    diagonal = jnp.broadcast_to(
        jnp.sum(jnp.where(eye, gram, 0.0), axis=1, keepdims=True), (16, 128))
    lengths = jnp.sqrt(jnp.maximum(diagonal, 0.0))
    beta = jnp.sqrt(jnp.broadcast_to(diagonal[0:1], (16, 128)) + epsilon)
    inverse = 1.0 / beta
    up_coef = jnp.where(sub2 == 1, HALF, HALF / 2)
    down_coef = jnp.where(sub2 < ITERS, HALF / 2, 0.0)
    g_lane = jnp.broadcast_to(gram[0:1], (16, 128)) * inverse
    c_lane = jnp.where(lane2 == 0, inverse, 0.0)
    g_sub = turned(g_lane)
    c_sub = jnp.where(sub2 == 0, inverse, 0.0)
    rest_t = jnp.where(eye, 1.0, 0.0) - g_sub * c_lane
    gram_rest_t = gram - g_sub * g_lane
    images = jnp.where(lane2 == 0, g_sub, 0.0)
    coords = [c_sub]
    trust = jnp.ones((16, 128), jnp.float32)

    cosines, sines, inverse_radii, upper = [], [], [], []
    target = [beta[0:1]]
    for j in range(ITERS):
        w_sub = (CENTER * c_sub + up_coef * pltpu.roll(c_sub, 1, 0)
                 + down_coef * pltpu.roll(c_sub, 15, 0))
        u_lane = down(rest_t * w_sub)
        gu_lane = down(gram_rest_t * w_sub)
        h_lane = down(images * w_sub)
        u_sub, gu_sub, h_sub = turned(u_lane), turned(gu_lane), turned(h_lane)
        square = down(u_sub * gu_sub)
        spread_square = down(jnp.abs(u_sub) * lengths)
        trust = jnp.where(square > TRUST * spread_square * spread_square, trust, 0.0)
        height = jnp.sqrt(jnp.maximum(square, 0.0) + epsilon)
        inverse = 1.0 / height
        if j + 1 < ITERS:
            c_sub, g_sub = u_sub * inverse, gu_sub * inverse
            c_lane, g_lane = u_lane * inverse, gu_lane * inverse
            rest_t = rest_t - g_sub * c_lane
            gram_rest_t = gram_rest_t - g_sub * g_lane
            images = jnp.where(lane2 == j + 1, g_sub, images)
            coords.append(c_sub)
        entries = [h_sub[i:i + 1] for i in range(j + 1)] + [height[0:1]]
        for row in range(j):
            entries[row], entries[row + 1] = (
                cosines[row] * entries[row] + sines[row] * entries[row + 1],
                cosines[row] * entries[row + 1] - sines[row] * entries[row])
        radius = jnp.sqrt(entries[j] * entries[j] + entries[j + 1] * entries[j + 1])
        inverse_radius = 1.0 / radius
        cosines.append(entries[j] * inverse_radius)
        sines.append(entries[j + 1] * inverse_radius)
        inverse_radii.append(inverse_radius)
        upper.append(entries[:j])
        lead = target[j]
        target[j] = cosines[j] * lead
        target.append(-sines[j] * lead)
    weights = [None] * ITERS
    for row in range(ITERS - 1, -1, -1):
        value = target[row]
        for later in range(ITERS - 1, row, -1):
            value = value - upper[later][row] * weights[later]
        weights[row] = value * inverse_radii[row]
    coef = weights[0] * coords[0]
    for j in range(1, ITERS):
        coef = coef + weights[j] * coords[j]
    flag[...] = trust[0:8]
    coefs = [jnp.broadcast_to(coef[k:k + 1], (8, 128)) for k in range(ITERS)]

    def combine(b, carry):
        for i in range(8):
            r = b * 8 + i
            value = coefs[0] * vecs[0, r]
            for k in range(1, ITERS):
                value = value + coefs[k] * vecs[k, r]
            tall[pl.ds(r, 8, stride=SHELLS), :] = value
        return carry

    lax.fori_loop(0, 8, combine, 0)
    sol = coefs[0] * planes[0, 0:8]
    sol_collector = coefs[0] * planes[0, 8:16]
    for k in range(1, ITERS):
        sol = sol + coefs[k] * planes[k, 0:8]
        sol_collector = sol_collector + coefs[k] * planes[k, 8:16]
    for g in range(4):
        block = tall[g * 128:(g + 1) * 128, :].T
        for q in range(4):
            at = (4 * q + g) * 128
            out_c[:, :, at:at + 128] = block[q * 32:(q + 1) * 32].reshape(2, 16, 128)
    by_node = [sol if q == 0 else pltpu.roll(sol, 128 - 32 * q, 1) for q in range(4)]
    by_node = jnp.concatenate(by_node + [sol_collector] + [jnp.zeros((88, 128), jnp.float32)], axis=0)
    out_p[...] = by_node.T[:CELLS, :CELLS + 1].reshape(2, 16, CELLS + 1)

    for k in range(ITERS):
        for d in range(4):
            @pl.when(sends[d][0])
            def _(k=k, d=d):
                halo_copy(k, d).wait_send()
    for step in range(1, n_a):
        copy_a(step)[1].wait_send()
    for step in range(1, n_b):
        copy_b(step)[1].wait_send()


def fast(nx, ny, *args):
    n_a, n_b = nx // 2, 2 * ny
    f32 = jnp.float32
    vmem = pl.BlockSpec(memory_space=pltpu.VMEM)
    return pl.pallas_call(
        functools.partial(kernel, nx, ny),
        out_shape=(
            jax.ShapeDtypeStruct(args[0].shape, f32),
            jax.ShapeDtypeStruct(args[1].shape, f32),
            jax.ShapeDtypeStruct((8, 128), f32),
        ),
        in_specs=[vmem] * 5,
        out_specs=(vmem,) * 3,
        scratch_shapes=[
            pltpu.VMEM((512, 128), f32),
            pltpu.VMEM((DIM, SHELLS, 8, 128), f32),
            pltpu.VMEM((DIM, 16, 128), f32),
            pltpu.VMEM((ITERS, 4, 16, 128), f32),
            pltpu.VMEM((128, 128), f32),
            pltpu.VMEM((n_a, 1, 128), f32),
            pltpu.VMEM((n_b, 1, 128), f32),
            pltpu.SemaphoreType.DMA((ITERS, 4)),
            pltpu.SemaphoreType.DMA((ITERS, 4)),
            pltpu.SemaphoreType.DMA((n_a,)),
            pltpu.SemaphoreType.DMA((n_a,)),
            pltpu.SemaphoreType.DMA((n_b,)),
            pltpu.SemaphoreType.DMA((n_b,)),
        ],
        compiler_params=pltpu.CompilerParams(collective_id=0, has_side_effects=True),
    )(*args)


def with_halo(shard, sides, width):
    edges = {}
    for axis, dim in sides:
        size, length = (lax.axis_size(axis), shard.shape[dim])
        up = [(i, (i + 1) % size) for i in range(size - 1)]
        last = lax.slice_in_dim(shard, length - width, length, axis=dim)
        initial = lax.slice_in_dim(shard, 0, width, axis=dim)
        edges[dim] = (
            lax.ppermute(last, axis, up),
            lax.ppermute(initial, axis, [(b, a) for a, b in up]),
        )
    done = []
    for _, dim in sides:
        low, high = edges[dim]
        around = [(width, width) if d in done else (0, 0) for d in range(shard.ndim)]
        shard = jnp.concatenate([jnp.pad(low, around), shard, jnp.pad(high, around)], axis=dim)
        done.append(dim)
    return shard


def total_of(shard):
    return lax.all_gather(shard, ("gx", "gy")).sum(axis=0)


def mirror_laplace(values):
    inner = jnp.concatenate([values[..., :1], values[..., :-1]], axis=-1)
    outer = jnp.concatenate([values[..., 1:], values[..., -1:]], axis=-1)
    return 2.0 * values - inner - outer


def local_operator(conc, padded, diffusion, exchange, slope):
    nodes = exchange.shape[2]
    shell_count = conc.shape[2] // nodes
    shells = conc.reshape(conc.shape[0], conc.shape[1], nodes, shell_count)
    center = padded[1:-1, 1:-1]
    lateral = (
        4.0 * center - padded[2:, 1:-1] - padded[:-2, 1:-1] - padded[1:-1, 2:] - padded[1:-1, :-2]
    )
    node_pot = center[..., :nodes]
    collector = center[..., nodes]
    current = exchange * (node_pot - collector[..., None])
    surface = shells[..., shell_count - 1]
    surface_flag = (lax.broadcasted_iota(jnp.int32, (shell_count,), 0) == shell_count - 1).astype(
        jnp.float32
    )
    new_shells = (
        shells + diffusion[..., None] * mirror_laplace(shells) + current[..., None] * surface_flag
    )
    new_nodes = (
        node_cond * mirror_laplace(node_pot)
        + current
        - slope * surface
        + plane_cond * lateral[..., :nodes]
    )
    new_collector = collector_cond * lateral[..., nodes] - jnp.mean(current, axis=-1)
    return (
        new_shells.reshape(conc.shape),
        jnp.concatenate([new_nodes, new_collector[..., None]], axis=-1),
    )


def step_by_step(rhs_conc, rhs_pots, diffusion, exchange, slope):
    first = jnp.sum(rhs_conc * rhs_conc) + jnp.sum(rhs_pots * rhs_pots)
    start_norm = jnp.sqrt(total_of(first.reshape(1))[0] + epsilon)
    all_conc = jnp.zeros((DIM, *rhs_conc.shape), jnp.float32).at[0].set(rhs_conc / start_norm)
    all_pots = jnp.zeros((DIM, *rhs_pots.shape), jnp.float32).at[0].set(rhs_pots / start_norm)
    matrix = jnp.zeros((DIM, DIM), jnp.float32)

    def arnoldi(step, state):
        all_conc, all_pots, matrix = state
        padded = with_halo(all_pots[step], (("gx", 0), ("gy", 1)), 1)
        image_conc, image_pots = local_operator(all_conc[step], padded, diffusion, exchange, slope)
        local_dots = jnp.sum(all_conc * image_conc, axis=(1, 2, 3)) + jnp.sum(
            all_pots * image_pots, axis=(1, 2, 3))
        coeffs = total_of(local_dots)
        rest_conc = image_conc - jnp.sum(coeffs[:, None, None, None] * all_conc, axis=0)
        rest_pots = image_pots - jnp.sum(coeffs[:, None, None, None] * all_pots, axis=0)
        rest = jnp.sum(rest_conc * rest_conc) + jnp.sum(rest_pots * rest_pots)
        height = jnp.sqrt(total_of(rest.reshape(1))[0] + epsilon)
        column = jnp.where(jnp.arange(DIM) == step + 1, height, coeffs)
        return (
            lax.dynamic_update_index_in_dim(all_conc, rest_conc / height, step + 1, 0),
            lax.dynamic_update_index_in_dim(all_pots, rest_pots / height, step + 1, 0),
            lax.dynamic_update_index_in_dim(matrix, column, step, 0),
        )

    all_conc, all_pots, matrix = lax.fori_loop(
        0, ITERS, arnoldi, (all_conc, all_pots, matrix))

    def rotate(step, state):
        matrix, target = state
        pair = matrix[step]
        lead, under = pair[step], pair[step + 1]
        radius = jnp.sqrt(lead * lead + under * under)
        cosine, sine = lead / radius, under / radius

        def turn(values):
            a = lax.dynamic_index_in_dim(values, step, values.ndim - 1)
            b = lax.dynamic_index_in_dim(values, step + 1, values.ndim - 1)
            values = lax.dynamic_update_slice_in_dim(
                values, cosine * a + sine * b, step, values.ndim - 1)
            return lax.dynamic_update_slice_in_dim(
                values, cosine * b - sine * a, step + 1, values.ndim - 1)

        return turn(matrix), turn(target)

    target = jnp.zeros((DIM,), jnp.float32).at[0].set(start_norm)
    matrix, target = lax.fori_loop(0, ITERS, rotate, (matrix, target))

    def back(i, weights):
        row = ITERS - 1 - i
        known = jnp.sum(matrix[:, row] * weights)
        return weights.at[row].set((target[row] - known) / matrix[row, row])

    weights = lax.fori_loop(0, ITERS, back, jnp.zeros((DIM,), jnp.float32))
    weights = weights[:, None, None, None]
    return jnp.sum(weights * all_conc, axis=0), jnp.sum(weights * all_pots, axis=0)


def solution(mesh):
    nx, ny = mesh.shape["gx"], mesh.shape["gy"]

    def shards(*args):
        conc, pots, flag = fast(nx, ny, *args)

        def again(state):
            conc, pots = step_by_step(*args)
            return conc, pots, jnp.ones_like(state[2])

        return lax.while_loop(
            lambda state: state[2] < 0.5, again, (conc, pots, jnp.min(flag)))[:2]

    spec = P("gx", "gy", None)
    return jax.shard_map(
        shards, mesh=mesh, in_specs=(spec,) * 5, out_specs=(spec,) * 2, check_vma=False)
```

profile of v0, /device:TPU:1, one launch (start us, length us, event | category | flops | bytes accessed | tf_op | source)
XLA Modules:
  0.0 63.9 jit_solution(3003050477652052638)
XLA Ops:
  0.6 58.0 %shard_map.68 = (f32[2,16,2048]{2,1,0:T(8,128)}, f32[2,16,33]{2,1,0:T(8,128)}, f32[8,128]{1,0:T(8,128)}) custom-call(f32[2,16,2048]{2,1,0:T(8,128)} %conc.1, f32[2,16,33]{2,1,0:T(8,128)} %pots.1, f32[2,16,32]{2,1,0:T(8,128)} %diff.1, f32[2,16,32]{2,1,0:T(8,128)} %exch.1, f32[2,16,32]{2,1,0:T(8,128)} %slope.1), custom_call_target="tpu_custom_call" | custom-call | tf_op jit(solution)/shard_map/pallas_call | solution.py:376
  58.6 1.4 %reduce_min.9 = f32[]{:T(128)} reduce(f32[8,128]{1,0:T(8,128)} %get-tuple-element.459, f32[]{:T(128)} %constant.385.clone.1), dimensions={0,1}, to_apply=%region_0.0 | reduce | flops 1023 | bytes 4104 | tf_op jit(solution)/shard_map/reduce_min | solution.py:534
  60.0 0.9 %while.61 = (f32[2,16,2048]{2,1,0:T(8,128)}, f32[2,16,33]{2,1,0:T(8,128)}, f32[]{:T(128)}, f32[2,16,2048]{2,1,0:T(8,128)}, f32[2,16,33]{2,1,0:T(8,128)}, /*index...) while((f32[2,16,2048]{2,1,0:T(8,128)}, f32[2,16,33]{2,1,0:T(8,128)}, f32[]{:T(128)}, ...), condition=%region_23.24_spmd, body=%region_1.23_spmd | while | flops 5886719 | bytes 25668336 | solution.py:533
  60.9 1.7 %copy.74 = f32[2,16,2048]{2,1,0:T(8,128)} copy(f32[2,16,2048]{2,1,0:T(8,128)} %get-tuple-element.806) | data formatting | bytes 524288
  62.6 1.3 %copy.75 = f32[2,16,33]{2,1,0:T(8,128)} copy(f32[2,16,33]{2,1,0:T(8,128)} %get-tuple-element.807) | data formatting | bytes 8448
where the time goes:
time: 64.1 us; the launch traced here: 63.9 us
  Pallas kernels  58 us (90%)
  local copies, waits for them, and re-layouts  2.99 us (5%)
  other arithmetic  1.37 us (2%)
  loops' own time  0.87 us (1%)
  between operations  0.65 us (1%)
    pallas_call x1, Pallas kernels, fast(): pl.pallas_call(functools.partial(kernel, nx, ny), out_shape=(jax.ShapeDty...  58 us
    unnamed x2, local copies, waits for them, and re-layouts  2.99 us
    reduce_min x1, other arithmetic, shards(): jnp.min(flag)  1.37 us

commit v1 on v0

--- a/solution.py
+++ b/solution.py
@@ -16,6 +16,7 @@
 collector_cond = 2.0
 epsilon = 1e-06
 
+ROUNDS = (5, 5)
 CENTER = 11.0
 HALF = 10.0
 TRUST = 1e-4
@@ -23,10 +24,39 @@
 CELLS = 32
 SHELLS = 64
 DIM = ITERS + 1
+STARTS = tuple(sum(ROUNDS[:i]) for i in range(len(ROUNDS)))
+
+
+def steps_away(block):
+    a, b = block
+    return max(2 * abs(a) - 1, 0) + abs(b)
+
+
+DEEPEST = max(ROUNDS)
+BLOCKS = sorted(
+    ((a, b) for a in range(-DEEPEST, DEEPEST + 1) for b in (-1, 0, 1)
+     if 0 < steps_away((a, b)) <= DEEPEST),
+    key=lambda block: (-steps_away(block), block))
+SLOT = {block: i for i, block in enumerate(BLOCKS)}
+COEFS = 24
+OUTBOX = 16 + COEFS + 8 * (DEEPEST - 1)
+
+
+def message_rows(turn, block):
+    updates = ROUNDS[turn] - steps_away(block)
+    if updates < 0:
+        return 0
+    if updates == 0:
+        return 16
+    return 16 + (COEFS if turn == 0 else 0) + 8 * updates
+
+
+def is_first(k):
+    return k in STARTS
 
 
 def kernel(nx, ny, conc, pots, diff, exch, slope, out_c, out_p, flag,
-           tall, vecs, planes, halo, rows, sums_a, sums_b,
+           tall, vecs, planes, outbox, halo, rows, sums_a, sums_b,
            hs_sem, hr_sem, as_sem, ar_sem, bs_sem, br_sem):
     n_a = nx // 2
     n_b = 2 * ny
@@ -45,23 +75,27 @@
         other = lax.rem(slot_b + step, n_b)
         return other, (col * 2 + lax.div(other, ny), lax.rem(other, ny))
 
-    sends = (
-        (gx < nx - 1, (gx + 1, gy)),
-        (gx > 0, (gx - 1, gy)),
-        (gy < ny - 1, (gx, gy + 1)),
-        (gy > 0, (gx, gy - 1)),
-    )
-    receives = (gx > 0, gx < nx - 1, gy > 0, gy < ny - 1)
+    exists = {}
+    for a, b in BLOCKS:
+        inside = []
+        if a:
+            inside.append(gx + a < nx if a > 0 else gx + a >= 0)
+        if b:
+            inside.append(gy + b < ny if b > 0 else gy + b >= 0)
+        exists[a, b] = inside[0] if len(inside) == 1 else jnp.logical_and(*inside)
 
     barrier = pltpu.get_barrier_semaphore()
-    for exists, device in sends:
-        @pl.when(exists)
-        def _(device=device):
-            pl.semaphore_signal(barrier, inc=1, device_id=device, device_id_type=MESH)
+    for step in range(1, n_b):
+        pl.semaphore_signal(barrier, inc=1, device_id=peer_b(step)[1], device_id_type=MESH)
     for step in range(1, n_a):
         pl.semaphore_signal(barrier, inc=1, device_id=peer_a(step)[1], device_id_type=MESH)
-    for step in range(1, n_b):
-        pl.semaphore_signal(barrier, inc=1, device_id=peer_b(step)[1], device_id_type=MESH)
+    expected = n_a + n_b - 2
+    for block in BLOCKS:
+        @pl.when(exists[block])
+        def _(block=block):
+            pl.semaphore_signal(
+                barrier, inc=1, device_id=(gx + block[0], gy + block[1]), device_id_type=MESH)
+        expected = expected + exists[block].astype(jnp.int32)
 
     lane = lax.broadcasted_iota(jnp.int32, (8, 128), 1)
     sub = lax.broadcasted_iota(jnp.int32, (8, 128), 0)
@@ -71,11 +105,13 @@
     once = jnp.logical_and(sub == 0, quarter == 0)
     zero = jnp.zeros((8, 128), jnp.float32)
 
-    for d in range(4):
-        @pl.when(jnp.logical_not(receives[d]))
-        def _(d=d):
-            for k in range(ITERS):
-                halo[k, d] = jnp.zeros((16, 128), jnp.float32)
+    for block in BLOCKS:
+        @pl.when(jnp.logical_not(exists[block]))
+        def _(block=block):
+            for turn in range(len(ROUNDS)):
+                count = message_rows(turn, block)
+                if count:
+                    halo[turn, SLOT[block], 0:count] = jnp.zeros((count, 128), jnp.float32)
 
     def spread(by_node):
         parts = [by_node[8 * q:8 * q + 8, :] for q in range(4)]
@@ -93,6 +129,11 @@
         jnp.concatenate([pots_t[CELLS:CELLS + 1]] * 4, axis=1), (8, 128))
     planes[0, 0:8] = pot
     planes[0, 8:16] = collector
+    outbox[0, 0:8] = pot
+    outbox[0, 8:16] = collector
+    outbox[0, 16:24] = exchange
+    outbox[0, 24:32] = slopes
+    outbox[0, 32:40] = diffusion
     rows[...] = jnp.zeros((128, 128), jnp.float32)
 
     flat = conc[...].reshape(CELLS, 2048)
@@ -100,6 +141,8 @@
         block = jnp.concatenate(
             [flat[:, (4 * q + g) * 128:(4 * q + g + 1) * 128] for q in range(4)], axis=0)
         tall[g * 128:(g + 1) * 128, :] = block.T
+    for i in range(ROUNDS[0] - 1):
+        outbox[0, 40 + 8 * i:48 + 8 * i] = tall[pl.ds(SHELLS - 1 - i, 8, stride=SHELLS), :]
 
     def first(b, acc):
         for i in range(8):
@@ -115,40 +158,53 @@
         if i != k:
             rows[DIM * i + k:DIM * i + k + 1, :] = total
 
+    def halo_copy(turn, block):
+        a, b = block
+        count = message_rows(turn, block)
+        return pltpu.make_async_remote_copy(
+            src_ref=outbox.at[turn, pl.ds(0, count)],
+            dst_ref=halo.at[turn, SLOT[-a, -b], pl.ds(0, count)],
+            send_sem=hs_sem.at[turn, SLOT[block]],
+            recv_sem=hr_sem.at[turn, SLOT[-a, -b]],
+            device_id=(gx + a, gy + b),
+            device_id_type=MESH,
+        )
+
+    def each_message(turn, act):
+        for block in BLOCKS:
+            if message_rows(turn, block):
+                @pl.when(exists[block])
+                def _(block=block):
+                    act(block)
+
+    def receive(turn, block):
+        a, b = block
+        count = message_rows(turn, block)
+        pltpu.make_async_remote_copy(
+            src_ref=outbox.at[turn, pl.ds(0, count)],
+            dst_ref=halo.at[turn, SLOT[block], pl.ds(0, count)],
+            send_sem=hs_sem.at[turn, SLOT[block]],
+            recv_sem=hr_sem.at[turn, SLOT[block]],
+            device_id=(gx + a, gy + b),
+            device_id_type=MESH,
+        ).wait_recv()
+
+    def send_round(turn):
+        each_message(turn, lambda block: halo_copy(turn, block).start())
+
+    pl.semaphore_wait(barrier, expected)
+    send_round(0)
     acc = lax.fori_loop(0, 8, first, zero)
     keep(0, 0, acc + pot * pot + jnp.where(once, collector * collector, 0.0))
 
-    pl.semaphore_wait(barrier, n_a + n_b - 2 + sum(r.astype(jnp.int32) for r in receives))
-
-    def halo_copy(k, d):
-        return pltpu.make_async_remote_copy(
-            src_ref=planes.at[k],
-            dst_ref=halo.at[k, d],
-            send_sem=hs_sem.at[k, d],
-            recv_sem=hr_sem.at[k, d],
-            device_id=sends[d][1],
-            device_id_type=MESH,
-        )
-
-    def send_halo(k):
-        for d in range(4):
-            @pl.when(sends[d][0])
-            def _(d=d):
-                halo_copy(k, d).start()
-
-    send_halo(0)
-
-    def lateral_inside(v):
-        return (4.0 * v
-                - jnp.where(x_of == 1, pltpu.roll(v, 16, 1), pltpu.roll(v, 112, 1))
-                - jnp.where(y_of > 0, pltpu.roll(v, 1, 1), 0.0)
-                - jnp.where(y_of < 15, pltpu.roll(v, 127, 1), 0.0))
-
-    def lateral_outside(k, at):
-        low_x, high_x, low_y, high_y = (halo[k, d, at:at + 8] for d in range(4))
-        return (jnp.where(x_of == 0, pltpu.roll(low_x, 112, 1), pltpu.roll(high_x, 16, 1))
-                + jnp.where(y_of == 0, pltpu.roll(low_y, 113, 1), 0.0)
-                + jnp.where(y_of == 15, pltpu.roll(high_y, 15, 1), 0.0))
+    def around(own, low_x, high_x, low_y, high_y):
+        high = own if high_x is None else own + high_x
+        low = own if low_x is None else own + low_x
+        before = 0.0 if low_y is None else pltpu.roll(low_y, 113, 1)
+        after = 0.0 if high_y is None else pltpu.roll(high_y, 15, 1)
+        return (jnp.where(x_of == 1, pltpu.roll(high, 16, 1), pltpu.roll(low, 112, 1))
+                + jnp.where(y_of > 0, pltpu.roll(own, 1, 1), before)
+                + jnp.where(y_of < 15, pltpu.roll(own, 127, 1), after))
 
     def node_mirror(v):
         down = pltpu.roll(v, 1, 0)
@@ -164,25 +220,84 @@
         v = v + pltpu.roll(v, 64, 1)
         return v + pltpu.roll(v, 32, 1)
 
-    for k in range(ITERS):
-        scale = (1.0 if k == 0 else 2.0) / HALF
-        pot = planes[k, 0:8]
-        collector = planes[k, 8:16]
-        current = exchange * (pot - collector)
-        own_pot = scale * (
-            node_cond * node_mirror(pot) + current - slopes * vecs[k, SHELLS - 1]
-            + plane_cond * lateral_inside(pot) - CENTER * pot)
-        own_collector = scale * (
-            collector_cond * lateral_inside(collector) - over_nodes(current) * (1.0 / 32.0)
-            - CENTER * collector)
-        if k > 0:
-            own_pot = own_pot - planes[k - 1, 0:8]
-            own_collector = own_collector - planes[k - 1, 8:16]
+    def potentials(turn):
+        depth, start = ROUNDS[turn], STARTS[turn]
+        carried = ROUNDS[turn + 1] - 1 if turn + 1 < len(ROUNDS) else 0
+        own = (0, 0)
+        now = {own: (planes[start, 0:8], planes[start, 8:16],
+                     [vecs[start, SHELLS - 1 - i] for i in range(depth + carried)])}
+        coefs = {own: (exchange, slopes, diffusion)}
+        for block in BLOCKS:
+            if message_rows(turn, block) == 0:
+                continue
+            updates = depth - steps_away(block)
+            inbox = halo.at[turn, SLOT[block]]
+            shells_at = 16 + (COEFS if turn == 0 else 0)
+            now[block] = (inbox[0:8], inbox[8:16],
+                          [inbox[shells_at + 8 * i:shells_at + 8 * i + 8] for i in range(updates)])
+            if updates:
+                source = halo.at[0, SLOT[block]]
+                coefs[block] = (source[16:24], source[24:32], source[32:40])
+        before = None
+        for m in range(1, depth + 1):
+            scale = (1.0 if m == 1 else 2.0) / HALF
+            after = {}
+            for block in now:
+                if steps_away(block) > depth - m:
+                    continue
+                a, b = block
+                pot, collector, shells = now[block]
+                exchange_of, slope_of, diffusion_of = coefs[block]
+                beside = [now.get(other) for other in (
+                    (a - 1, b), (a + 1, b), (a, b - 1), (a, b + 1))]
+
+                def lateral(which, own):
+                    return 4.0 * own - around(
+                        own, *(None if other is None else other[which] for other in beside))
+
+                current = exchange_of * (pot - collector)
+                new_pot = scale * (
+                    node_cond * node_mirror(pot) + current - slope_of * shells[0]
+                    + plane_cond * lateral(0, pot) - CENTER * pot)
+                new_collector = scale * (
+                    collector_cond * lateral(1, collector)
+                    - over_nodes(current) * (1.0 / 32.0) - CENTER * collector)
+                count = depth - m + carried if block == own_block else depth - steps_away(block) - m
+                center_coef = scale * (1.0 - CENTER + 2.0 * diffusion_of)
+                side_coef = scale * diffusion_of
+                new_shells = []
+                for i in range(count):
+                    new = center_coef * shells[i] - side_coef * (shells[max(i - 1, 0)] + shells[i + 1])
+                    if i == 0:
+                        new = new + scale * current
+                    if m > 1:
+                        new = new - before[block][2][i]
+                    new_shells.append(new)
+                if m > 1:
+                    new_pot = new_pot - before[block][0]
+                    new_collector = new_collector - before[block][1]
+                if block != own_block:
+                    new_pot = jnp.where(exists[block], new_pot, 0.0)
+                    new_collector = jnp.where(exists[block], new_collector, 0.0)
+                after[block] = (new_pot, new_collector, new_shells)
+            planes[start + m, 0:8] = after[own_block][0]
+            planes[start + m, 8:16] = after[own_block][1]
+            before, now = now, after
+        if turn + 1 < len(ROUNDS):
+            outbox[turn + 1, 0:8] = now[own_block][0]
+            outbox[turn + 1, 8:16] = now[own_block][1]
+            for i in range(carried):
+                outbox[turn + 1, 16 + 8 * i:24 + 8 * i] = now[own_block][2][i]
+
+    own_block = (0, 0)
+
+    def bulk_shells(k):
+        scale = (1.0 if is_first(k) else 2.0) / HALF
+        current = exchange * (planes[k, 0:8] - planes[k, 8:16])
         center_coef = scale * (1.0 - CENTER + 2.0 * diffusion)
         side_coef = scale * diffusion
 
-        def shells(base, accs, last, k=k, center_coef=center_coef, side_coef=side_coef,
-                   scale=scale, current=current):
+        def shells(base, accs, last):
             accs = list(accs)
             low = vecs[k, jnp.maximum(base - 1, 0)]
             here = vecs[k, base]
@@ -192,7 +307,7 @@
                 new = center_coef * here - side_coef * (low + high)
                 if last and i == 7:
                     new = new + scale * current
-                if k > 0:
+                if not is_first(k):
                     new = new - vecs[k - 1, r]
                 vecs[k + 1, r] = new
                 for m in range(k):
@@ -204,22 +319,24 @@
 
         accs = lax.fori_loop(
             0, 7, lambda b, accs: shells(b * 8, accs, False), (zero,) * (k + 2))
-        accs = shells(SHELLS - 8, accs, True)
-
-        for d in range(4):
-            @pl.when(receives[d])
-            def _(d=d):
-                halo_copy(k, d).wait_recv()
-        new_pot = own_pot - (scale * plane_cond) * lateral_outside(k, 0)
-        new_collector = own_collector - (scale * collector_cond) * lateral_outside(k, 8)
-        planes[k + 1, 0:8] = new_pot
-        planes[k + 1, 8:16] = new_collector
-        if k + 1 < ITERS:
-            send_halo(k + 1)
+        return shells(SHELLS - 8, accs, True)
+
+    def products(k, accs):
+        new_pot, new_collector = planes[k + 1, 0:8], planes[k + 1, 8:16]
         for m in range(k + 2):
             acc = accs[m] + new_pot * planes[m, 0:8] + jnp.where(
                 once, new_collector * planes[m, 8:16], 0.0)
             keep(k + 1, m, acc)
+
+    for turn, start in enumerate(STARTS):
+        accs = bulk_shells(start)
+        each_message(turn, functools.partial(receive, turn))
+        potentials(turn)
+        if turn + 1 < len(ROUNDS):
+            send_round(turn + 1)
+        products(start, accs)
+        for k in range(start + 1, start + ROUNDS[turn]):
+            products(k, bulk_shells(k))
 
     def total(mine, count, slot, peer, sums, s_sem, r_sem):
         sums[pl.ds(slot, 1)] = mine.reshape(1, 1, 128)
@@ -275,8 +392,12 @@
     lengths = jnp.sqrt(jnp.maximum(diagonal, 0.0))
     beta = jnp.sqrt(jnp.broadcast_to(diagonal[0:1], (16, 128)) + epsilon)
     inverse = 1.0 / beta
-    up_coef = jnp.where(sub2 == 1, HALF, HALF / 2)
-    down_coef = jnp.where(sub2 < ITERS, HALF / 2, 0.0)
+    up_coef = jnp.zeros((16, 128), jnp.float32)
+    down_coef = jnp.zeros((16, 128), jnp.float32)
+    for k in range(ITERS):
+        up_coef = jnp.where(sub2 == k + 1, HALF if is_first(k) else HALF / 2, up_coef)
+        if not is_first(k):
+            down_coef = jnp.where(sub2 == k - 1, HALF / 2, down_coef)
     g_lane = jnp.broadcast_to(gram[0:1], (16, 128)) * inverse
     c_lane = jnp.where(lane2 == 0, inverse, 0.0)
     g_sub = turned(g_lane)
@@ -358,11 +479,8 @@
     by_node = jnp.concatenate(by_node + [sol_collector] + [jnp.zeros((88, 128), jnp.float32)], axis=0)
     out_p[...] = by_node.T[:CELLS, :CELLS + 1].reshape(2, 16, CELLS + 1)
 
-    for k in range(ITERS):
-        for d in range(4):
-            @pl.when(sends[d][0])
-            def _(k=k, d=d):
-                halo_copy(k, d).wait_send()
+    for turn in range(len(ROUNDS)):
+        each_message(turn, lambda block: halo_copy(turn, block).wait_send())
     for step in range(1, n_a):
         copy_a(step)[1].wait_send()
     for step in range(1, n_b):
@@ -386,12 +504,13 @@
             pltpu.VMEM((512, 128), f32),
             pltpu.VMEM((DIM, SHELLS, 8, 128), f32),
             pltpu.VMEM((DIM, 16, 128), f32),
-            pltpu.VMEM((ITERS, 4, 16, 128), f32),
+            pltpu.VMEM((len(ROUNDS), OUTBOX, 128), f32),
+            pltpu.VMEM((len(ROUNDS), len(BLOCKS), OUTBOX, 128), f32),
             pltpu.VMEM((128, 128), f32),
             pltpu.VMEM((n_a, 1, 128), f32),
             pltpu.VMEM((n_b, 1, 128), f32),
-            pltpu.SemaphoreType.DMA((ITERS, 4)),
-            pltpu.SemaphoreType.DMA((ITERS, 4)),
+            pltpu.SemaphoreType.DMA((len(ROUNDS), len(BLOCKS))),
+            pltpu.SemaphoreType.DMA((len(ROUNDS), len(BLOCKS))),
             pltpu.SemaphoreType.DMA((n_a,)),
             pltpu.SemaphoreType.DMA((n_a,)),
             pltpu.SemaphoreType.DMA((n_b,)),

time: 64.1 us -> 45.2 us (0.71)
  Pallas kernels: 58 us -> 39.1 us
    pallas_call x1, Pallas kernels: 58 us -> 39.1 us  [fast(): pl.pallas_call(functools.partial(kernel, nx, ny), out_shape=(jax.ShapeDty...]
where the time goes in v1:
time: 45.2 us; the launch traced here: 45 us
  Pallas kernels  39.1 us (87%)
  local copies, waits for them, and re-layouts  2.99 us (7%)
  other arithmetic  1.37 us (3%)
  loops' own time  0.87 us (2%)
  between operations  0.65 us (1%)
    pallas_call x1, Pallas kernels, fast(): pl.pallas_call(functools.partial(kernel, nx, ny), out_shape=(jax.ShapeDty...  39.1 us
    unnamed x2, local copies, waits for them, and re-layouts  2.99 us
    reduce_min x1, other arithmetic, shards(): jnp.min(flag)  1.37 us

profile of v1, /device:TPU:1, one launch (start us, length us, event | category | flops | bytes accessed | tf_op | source)
XLA Modules:
  0.0 45.0 jit_solution(9665119048401693999)
XLA Ops:
  0.6 39.1 %shard_map.68 = (f32[2,16,2048]{2,1,0:T(8,128)}, f32[2,16,33]{2,1,0:T(8,128)}, f32[8,128]{1,0:T(8,128)}) custom-call(f32[2,16,2048]{2,1,0:T(8,128)} %conc.1, f32[2,16,33]{2,1,0:T(8,128)} %pots.1, f32[2,16,32]{2,1,0:T(8,128)} %diff.1, f32[2,16,32]{2,1,0:T(8,128)} %exch.1, f32[2,16,32]{2,1,0:T(8,128)} %slope.1), custom_call_target="tpu_custom_call" | custom-call | tf_op jit(solution)/shard_map/pallas_call | solution.py:494
  39.7 1.4 %reduce_min.9 = f32[]{:T(128)} reduce(f32[8,128]{1,0:T(8,128)} %get-tuple-element.459, f32[]{:T(128)} %constant.385.clone.1), dimensions={0,1}, to_apply=%region_0.0 | reduce | flops 1023 | bytes 4104 | tf_op jit(solution)/shard_map/reduce_min | solution.py:653
  41.1 0.9 %while.61 = (f32[2,16,2048]{2,1,0:T(8,128)}, f32[2,16,33]{2,1,0:T(8,128)}, f32[]{:T(128)}, f32[2,16,2048]{2,1,0:T(8,128)}, f32[2,16,33]{2,1,0:T(8,128)}, /*index...) while((f32[2,16,2048]{2,1,0:T(8,128)}, f32[2,16,33]{2,1,0:T(8,128)}, f32[]{:T(128)}, ...), condition=%region_23.24_spmd, body=%region_1.23_spmd | while | flops 5886719 | bytes 25668336 | solution.py:652
  42.0 1.7 %copy.74 = f32[2,16,2048]{2,1,0:T(8,128)} copy(f32[2,16,2048]{2,1,0:T(8,128)} %get-tuple-element.806) | data formatting | bytes 524288
  43.6 1.3 %copy.75 = f32[2,16,33]{2,1,0:T(8,128)} copy(f32[2,16,33]{2,1,0:T(8,128)} %get-tuple-element.807) | data formatting | bytes 8448

commit v2 on v1

--- a/solution.py
+++ b/solution.py
@@ -55,7 +55,7 @@
     return k in STARTS
 
 
-def kernel(nx, ny, conc, pots, diff, exch, slope, out_c, out_p, flag,
+def kernel(nx, ny, conc, pots, diff, exch, slope, tall_out, plane_out, flag,
            tall, vecs, planes, outbox, halo, rows, sums_a, sums_b,
            hs_sem, hr_sem, as_sem, ar_sem, bs_sem, br_sem):
     n_a = nx // 2
@@ -452,7 +452,7 @@
     coef = weights[0] * coords[0]
     for j in range(1, ITERS):
         coef = coef + weights[j] * coords[j]
-    flag[...] = trust[0:8]
+    flag[0, 0] = jnp.min(trust)
     coefs = [jnp.broadcast_to(coef[k:k + 1], (8, 128)) for k in range(ITERS)]
 
     def combine(b, carry):
@@ -461,7 +461,7 @@
             value = coefs[0] * vecs[0, r]
             for k in range(1, ITERS):
                 value = value + coefs[k] * vecs[k, r]
-            tall[pl.ds(r, 8, stride=SHELLS), :] = value
+            tall_out[pl.ds(r, 8, stride=SHELLS), :] = value
         return carry
 
     lax.fori_loop(0, 8, combine, 0)
@@ -470,14 +470,8 @@
     for k in range(1, ITERS):
         sol = sol + coefs[k] * planes[k, 0:8]
         sol_collector = sol_collector + coefs[k] * planes[k, 8:16]
-    for g in range(4):
-        block = tall[g * 128:(g + 1) * 128, :].T
-        for q in range(4):
-            at = (4 * q + g) * 128
-            out_c[:, :, at:at + 128] = block[q * 32:(q + 1) * 32].reshape(2, 16, 128)
-    by_node = [sol if q == 0 else pltpu.roll(sol, 128 - 32 * q, 1) for q in range(4)]
-    by_node = jnp.concatenate(by_node + [sol_collector] + [jnp.zeros((88, 128), jnp.float32)], axis=0)
-    out_p[...] = by_node.T[:CELLS, :CELLS + 1].reshape(2, 16, CELLS + 1)
+    plane_out[0:8] = sol
+    plane_out[8:16] = sol_collector
 
     for turn in range(len(ROUNDS)):
         each_message(turn, lambda block: halo_copy(turn, block).wait_send())
@@ -487,19 +481,32 @@
         copy_b(step)[1].wait_send()
 
 
+def results(tall, planes, out_c, out_p):
+    for g in range(4):
+        block = tall[g * 128:(g + 1) * 128, :].T
+        for q in range(4):
+            at = (4 * q + g) * 128
+            out_c[:, :, at:at + 128] = block[q * 32:(q + 1) * 32].reshape(2, 16, 128)
+    sol = planes[0:8]
+    by_node = [sol if q == 0 else pltpu.roll(sol, 128 - 32 * q, 1) for q in range(4)]
+    by_node = jnp.concatenate(
+        by_node + [planes[8:16], jnp.zeros((88, 128), jnp.float32)], axis=0)
+    out_p[...] = by_node.T[:CELLS, :CELLS + 1].reshape(2, 16, CELLS + 1)
+
+
 def fast(nx, ny, *args):
     n_a, n_b = nx // 2, 2 * ny
     f32 = jnp.float32
     vmem = pl.BlockSpec(memory_space=pltpu.VMEM)
-    return pl.pallas_call(
+    tall, planes, flag = pl.pallas_call(
         functools.partial(kernel, nx, ny),
         out_shape=(
-            jax.ShapeDtypeStruct(args[0].shape, f32),
-            jax.ShapeDtypeStruct(args[1].shape, f32),
-            jax.ShapeDtypeStruct((8, 128), f32),
+            pltpu.VMEM((512, 128), f32),
+            pltpu.VMEM((16, 128), f32),
+            jax.ShapeDtypeStruct((1, 1), f32),
         ),
         in_specs=[vmem] * 5,
-        out_specs=(vmem,) * 3,
+        out_specs=(vmem, vmem, pl.BlockSpec(memory_space=pltpu.SMEM)),
         scratch_shapes=[
             pltpu.VMEM((512, 128), f32),
             pltpu.VMEM((DIM, SHELLS, 8, 128), f32),
@@ -518,6 +525,13 @@
         ],
         compiler_params=pltpu.CompilerParams(collective_id=0, has_side_effects=True),
     )(*args)
+    conc, pots = pl.pallas_call(
+        results,
+        out_shape=tuple(jax.ShapeDtypeStruct(a.shape, f32) for a in args[:2]),
+        in_specs=[vmem] * 2,
+        out_specs=(vmem,) * 2,
+    )(*(pltpu.with_memory_space_constraint(a, pltpu.VMEM) for a in (tall, planes)))
+    return conc, pots, flag
 
 
 def with_halo(shard, sides, width):
@@ -650,7 +664,7 @@
             return conc, pots, jnp.ones_like(state[2])
 
         return lax.while_loop(
-            lambda state: state[2] < 0.5, again, (conc, pots, jnp.min(flag)))[:2]
+            lambda state: state[2] < 0.5, again, (conc, pots, flag[0, 0]))[:2]
 
     spec = P("gx", "gy", None)
     return jax.shard_map(

time: 45.2 us -> 41.3 us (0.914)
  local copies, waits for them, and re-layouts: 2.99 us -> 0 us
  other arithmetic: 1.37 us -> 0 us
  Pallas kernels: 39.1 us -> 39.6 us
    unnamed x2 -> x0, local copies, waits for them, and re-layouts: 2.99 us -> none
    reduce_min x1 -> x0, other arithmetic: 1.37 us -> none  [shards(): jnp.min(flag)]
    pallas_call x1 -> x2, Pallas kernels: 39.1 us -> 39.6 us  [the longest x1 38.8 us: fast(): pl.pallas_call(functools.partial(kernel, nx, ny), out_shape=(pltpu.VMEM((...]
where the time goes in v2:
time: 41.3 us; the launch traced here: 41.2 us
  Pallas kernels  39.6 us (96%)
  between operations  0.8 us (2%)
  loops' own time  0.75 us (2%)
    pallas_call x1, Pallas kernels, fast(): pl.pallas_call(functools.partial(kernel, nx, ny), out_shape=(pltpu.VMEM((...  38.8 us
    pallas_call x1, Pallas kernels, fast(): pl.pallas_call(results, out_shape=tuple((jax.ShapeDtypeStruct(a.shape, f3...  0.86 us

profile of v2, /device:TPU:1, one launch (start us, length us, event | category | flops | bytes accessed | tf_op | source)
XLA Modules:
  0.0 41.2 jit_solution(14735728875531181717)
XLA Ops:
  0.6 38.8 %shard_map.68 = (f32[512,128]{1,0:T(8,128)S(1)}, f32[16,128]{1,0:T(8,128)S(1)}, f32[1,1]{1,0:T(1,128)}) custom-call(f32[2,16,2048]{2,1,0:T(8,128)} %conc.1, f32[2,16,33]{2,1,0:T(8,128)} %pots.1, f32[2,16,32]{2,1,0:T(8,128)} %diff.1, f32[2,16,32]{2,1,0:T(8,128)} %exch.1, f32[2,16,32]{2,1,0:T(8,128)} %slope.1), custom_call_target="tpu_custom_call" | custom-call | tf_op jit(solution)/shard_map/pallas_call | solution.py:501
  39.4 0.9 %shard_map.69 = (f32[2,16,2048]{2,1,0:T(8,128)}, f32[2,16,33]{2,1,0:T(8,128)}) custom-call(f32[512,128]{1,0:T(8,128)S(1)} %get-tuple-element.459.tall, f32[16,128]{1,0:T(8,128)S(1)} %get-tuple-element.460.planes), custom_call_target="tpu_custom_call" | custom-call | tf_op jit(solution)/shard_map/pallas_call | solution.py:528
  40.3 0.7 %while.61 = (f32[2,16,2048]{2,1,0:T(8,128)}, f32[2,16,33]{2,1,0:T(8,128)}, f32[]{:T(128)}, f32[2,16,2048]{2,1,0:T(8,128)}, f32[2,16,33]{2,1,0:T(8,128)}, /*index...) while((f32[2,16,2048]{2,1,0:T(8,128)}, f32[2,16,33]{2,1,0:T(8,128)}, f32[]{:T(128)}, ...), condition=%region_22.23_spmd, body=%region_0.22_spmd | while | flops 5886719 | bytes 25668336 | solution.py:666

commit v3 on v2

--- a/solution.py
+++ b/solution.py
@@ -46,18 +46,41 @@
     updates = ROUNDS[turn] - steps_away(block)
     if updates < 0:
         return 0
+    if block[1]:
+        return 8 * len(fields_of(turn, updates))
     if updates == 0:
         return 16
     return 16 + (COEFS if turn == 0 else 0) + 8 * updates
 
 
+WIDE = 5
+assert DEEPEST <= WIDE
+
+
+def fields_of(turn, updates):
+    names = ["pots"]
+    if updates and turn == 0:
+        names.append("coefs")
+    if updates > 1:
+        names.append("shells")
+    return names
+
+
 def is_first(k):
     return k in STARTS
 
 
-def kernel(nx, ny, conc, pots, diff, exch, slope, tall_out, plane_out, flag,
+def kernel(nx, ny, conc_in, pots_in, diff_in, exch_in, slope_in, tall_out, plane_out, flag,
            tall, vecs, planes, outbox, halo, rows, sums_a, sums_b,
-           hs_sem, hr_sem, as_sem, ar_sem, bs_sem, br_sem):
+           hs_sem, hr_sem, as_sem, ar_sem, bs_sem, br_sem,
+           conc, pots, diff, exch, slope, in_sem):
+    loads = [
+        pltpu.make_async_copy(source, target, in_sem.at[i])
+        for i, (source, target) in enumerate((
+            (conc_in, conc), (diff_in, diff), (exch_in, exch), (slope_in, slope), (pots_in, pots)))]
+    for load in loads:
+        load.start()
+
     n_a = nx // 2
     n_b = 2 * ny
     gx = lax.axis_index("gx")
@@ -120,6 +143,8 @@
     def small(ref):
         return spread(ref[...].reshape(CELLS, CELLS).T)
 
+    for load in loads:
+        load.wait()
     diffusion = small(diff)
     exchange = small(exch)
     slopes = small(slope)
@@ -129,11 +154,6 @@
         jnp.concatenate([pots_t[CELLS:CELLS + 1]] * 4, axis=1), (8, 128))
     planes[0, 0:8] = pot
     planes[0, 8:16] = collector
-    outbox[0, 0:8] = pot
-    outbox[0, 8:16] = collector
-    outbox[0, 16:24] = exchange
-    outbox[0, 24:32] = slopes
-    outbox[0, 32:40] = diffusion
     rows[...] = jnp.zeros((128, 128), jnp.float32)
 
     flat = conc[...].reshape(CELLS, 2048)
@@ -141,8 +161,36 @@
         block = jnp.concatenate(
             [flat[:, (4 * q + g) * 128:(4 * q + g + 1) * 128] for q in range(4)], axis=0)
         tall[g * 128:(g + 1) * 128, :] = block.T
-    for i in range(ROUNDS[0] - 1):
-        outbox[0, 40 + 8 * i:48 + 8 * i] = tall[pl.ds(SHELLS - 1 - i, 8, stride=SHELLS), :]
+
+    def pack(fields, side):
+        start = 16 - WIDE if side == 1 else 0
+        packed = zero
+        for i, field in enumerate(fields):
+            shift = (WIDE * i - start) % 128
+            moved = pltpu.roll(field, shift, 1) if shift else field
+            packed = jnp.where(jnp.logical_and(y_of >= WIDE * i, y_of < WIDE * (i + 1)), moved, packed)
+        return packed
+
+    def unpack(packed, i, side):
+        start = 16 - WIDE if side == 1 else 0
+        shift = (start - WIDE * i) % 128
+        return pltpu.roll(packed, shift, 1) if shift else packed
+
+    def fill_outbox(turn, pot, collector, shells, coefs):
+        for i, field in enumerate([pot, collector] + coefs + shells):
+            outbox[turn, 0, 8 * i:8 * i + 8] = field
+        for side in (1, -1):
+            fields = [pack([pot, collector] + shells[:1], side)]
+            if coefs:
+                fields.append(pack(coefs, side))
+            if len(shells) > 1:
+                fields.append(pack(shells[1:], side))
+            for i, field in enumerate(fields):
+                outbox[turn, side % 3, 8 * i:8 * i + 8] = field
+
+    fill_outbox(0, pot, collector,
+                [tall[pl.ds(SHELLS - 1 - i, 8, stride=SHELLS), :] for i in range(ROUNDS[0] - 1)],
+                [exchange, slopes, diffusion])
 
     def first(b, acc):
         for i in range(8):
@@ -162,7 +210,7 @@
         a, b = block
         count = message_rows(turn, block)
         return pltpu.make_async_remote_copy(
-            src_ref=outbox.at[turn, pl.ds(0, count)],
+            src_ref=outbox.at[turn, b % 3, pl.ds(0, count)],
             dst_ref=halo.at[turn, SLOT[-a, -b], pl.ds(0, count)],
             send_sem=hs_sem.at[turn, SLOT[block]],
             recv_sem=hr_sem.at[turn, SLOT[-a, -b]],
@@ -181,7 +229,7 @@
         a, b = block
         count = message_rows(turn, block)
         pltpu.make_async_remote_copy(
-            src_ref=outbox.at[turn, pl.ds(0, count)],
+            src_ref=outbox.at[turn, b % 3, pl.ds(0, count)],
             dst_ref=halo.at[turn, SLOT[block], pl.ds(0, count)],
             send_sem=hs_sem.at[turn, SLOT[block]],
             recv_sem=hr_sem.at[turn, SLOT[block]],
@@ -217,8 +265,7 @@
 
     def over_nodes(v):
         v = jnp.broadcast_to(jnp.sum(v, axis=0, keepdims=True), (8, 128))
-        v = v + pltpu.roll(v, 64, 1)
-        return v + pltpu.roll(v, 32, 1)
+        return (v + pltpu.roll(v, 32, 1)) + (pltpu.roll(v, 64, 1) + pltpu.roll(v, 96, 1))
 
     def potentials(turn):
         depth, start = ROUNDS[turn], STARTS[turn]
@@ -232,6 +279,17 @@
                 continue
             updates = depth - steps_away(block)
             inbox = halo.at[turn, SLOT[block]]
+            if block[1]:
+                side = -block[1]
+                names = fields_of(turn, updates)
+                found = {name: inbox[8 * i:8 * i + 8] for i, name in enumerate(names)}
+                shells = [unpack(found["pots"], 2, side)] if updates else []
+                shells += [unpack(found["shells"], i, side) for i in range(updates - 1)]
+                now[block] = (unpack(found["pots"], 0, side), unpack(found["pots"], 1, side), shells)
+                if updates:
+                    source = halo[0, SLOT[block], 8:16]
+                    coefs[block] = tuple(unpack(source, i, side) for i in range(3))
+                continue
             shells_at = 16 + (COEFS if turn == 0 else 0)
             now[block] = (inbox[0:8], inbox[8:16],
                           [inbox[shells_at + 8 * i:shells_at + 8 * i + 8] for i in range(updates)])
@@ -284,10 +342,7 @@
             planes[start + m, 8:16] = after[own_block][1]
             before, now = now, after
         if turn + 1 < len(ROUNDS):
-            outbox[turn + 1, 0:8] = now[own_block][0]
-            outbox[turn + 1, 8:16] = now[own_block][1]
-            for i in range(carried):
-                outbox[turn + 1, 16 + 8 * i:24 + 8 * i] = now[own_block][2][i]
+            fill_outbox(turn + 1, *now[own_block], [])
 
     own_block = (0, 0)
 
@@ -505,13 +560,13 @@
             pltpu.VMEM((16, 128), f32),
             jax.ShapeDtypeStruct((1, 1), f32),
         ),
-        in_specs=[vmem] * 5,
+        in_specs=[pl.BlockSpec(memory_space=pltpu.HBM)] * 5,
         out_specs=(vmem, vmem, pl.BlockSpec(memory_space=pltpu.SMEM)),
         scratch_shapes=[
             pltpu.VMEM((512, 128), f32),
             pltpu.VMEM((DIM, SHELLS, 8, 128), f32),
             pltpu.VMEM((DIM, 16, 128), f32),
-            pltpu.VMEM((len(ROUNDS), OUTBOX, 128), f32),
+            pltpu.VMEM((len(ROUNDS), 3, OUTBOX, 128), f32),
             pltpu.VMEM((len(ROUNDS), len(BLOCKS), OUTBOX, 128), f32),
             pltpu.VMEM((128, 128), f32),
             pltpu.VMEM((n_a, 1, 128), f32),
@@ -522,6 +577,8 @@
             pltpu.SemaphoreType.DMA((n_a,)),
             pltpu.SemaphoreType.DMA((n_b,)),
             pltpu.SemaphoreType.DMA((n_b,)),
+            *(pltpu.VMEM(a.shape, f32) for a in args),
+            pltpu.SemaphoreType.DMA((5,)),
         ],
         compiler_params=pltpu.CompilerParams(collective_id=0, has_side_effects=True),
     )(*args)

time: 41.3 us -> 39.2 us (0.949)
  Pallas kernels: 39.6 us -> 37.6 us
    pallas_call x1, Pallas kernels: 38.8 us -> 36.7 us  [fast(): pl.pallas_call(functools.partial(kernel, nx, ny), out_shape=(pltpu.VMEM((...]
where the time goes in v3:
time: 39.2 us; the launch traced here: 39.1 us
  Pallas kernels  37.6 us (96%)
  between operations  0.8 us (2%)
  loops' own time  0.75 us (2%)
    pallas_call x1, Pallas kernels, fast(): pl.pallas_call(functools.partial(kernel, nx, ny), out_shape=(pltpu.VMEM((...  36.7 us
    pallas_call x1, Pallas kernels, fast(): pl.pallas_call(results, out_shape=tuple((jax.ShapeDtypeStruct(a.shape, f3...  0.86 us

profile of v3, /device:TPU:1, one launch (start us, length us, event | category | flops | bytes accessed | tf_op | source)
XLA Modules:
  0.0 39.1 jit_solution(770089872439648325)
XLA Ops:
  0.6 36.7 %shard_map.68 = (f32[512,128]{1,0:T(8,128)S(1)}, f32[16,128]{1,0:T(8,128)S(1)}, f32[1,1]{1,0:T(1,128)}) custom-call(f32[2,16,2048]{2,1,0:T(8,128)} %conc_in.1, f32[2,16,33]{2,1,0:T(8,128)} %pots_in.1, f32[2,16,32]{2,1,0:T(8,128)} %diff_in.1, f32[2,16,32]{2,1,0:T(8,128)} %exch_in.1, f32[2,16,32]{2,1,0:T(8,128)} %slope_in.1), custom_call_target="tpu_custom_call" | custom-call | tf_op jit(solution)/shard_map/pallas_call | solution.py:556
  37.3 0.9 %shard_map.69 = (f32[2,16,2048]{2,1,0:T(8,128)}, f32[2,16,33]{2,1,0:T(8,128)}) custom-call(f32[512,128]{1,0:T(8,128)S(1)} %get-tuple-element.459.tall, f32[16,128]{1,0:T(8,128)S(1)} %get-tuple-element.460.planes), custom_call_target="tpu_custom_call" | custom-call | tf_op jit(solution)/shard_map/pallas_call | solution.py:585
  38.2 0.7 %while.61 = (f32[2,16,2048]{2,1,0:T(8,128)}, f32[2,16,33]{2,1,0:T(8,128)}, f32[]{:T(128)}, f32[2,16,2048]{2,1,0:T(8,128)}, f32[2,16,33]{2,1,0:T(8,128)}, /*index...) while((f32[2,16,2048]{2,1,0:T(8,128)}, f32[2,16,33]{2,1,0:T(8,128)}, f32[]{:T(128)}, ...), condition=%region_22.23_spmd, body=%region_0.22_spmd | while | flops 5886719 | bytes 25668336 | solution.py:723

commit v4 on v3

--- a/solution.py
+++ b/solution.py
@@ -66,14 +66,50 @@
     return names
 
 
+STAGES = (("core",), ("z",), ("x", "y"))
+
+
+def extents(nx, ny):
+    columns = min(4, nx // 2)
+    return {"x": nx // 2 // columns, "y": columns, "core": 2, "z": ny}
+
+
+def members(names, nx, ny):
+    count = 1
+    for name in names:
+        count *= extents(nx, ny)[name]
+    return count
+
+
+class Group:
+    def __init__(self, names, nx, ny, gx, gy):
+        self.names, self.extents = names, extents(nx, ny)
+        columns = self.extents["y"]
+        self.place = {"core": lax.rem(gx, 2), "y": lax.rem(lax.div(gx, 2), columns),
+                      "x": lax.div(gx, 2 * columns), "z": gy}
+        self.count = members(names, nx, ny)
+        self.slot = 0
+        for name in names:
+            self.slot = self.slot * self.extents[name] + self.place[name]
+
+    def peer(self, step):
+        other = lax.rem(self.slot + step, self.count)
+        place, left = dict(self.place), other
+        for name in reversed(self.names):
+            place[name] = lax.rem(left, self.extents[name])
+            left = lax.div(left, self.extents[name])
+        row = (place["x"] * self.extents["y"] + place["y"]) * 2 + place["core"]
+        return other, (row, place["z"])
+
+
 def is_first(k):
     return k in STARTS
 
 
 def kernel(nx, ny, conc_in, pots_in, diff_in, exch_in, slope_in, tall_out, plane_out, flag,
-           tall, vecs, planes, outbox, halo, rows, sums_a, sums_b,
-           hs_sem, hr_sem, as_sem, ar_sem, bs_sem, br_sem,
-           conc, pots, diff, exch, slope, in_sem):
+           tall, vecs, planes, outbox, halo, rows, conc, pots, diff, exch, slope, hs_sem, hr_sem, in_sem,
+           *for_sums):
+    sums, sum_sems = for_sums[:len(STAGES)], for_sums[len(STAGES):]
     loads = [
         pltpu.make_async_copy(source, target, in_sem.at[i])
         for i, (source, target) in enumerate((
@@ -81,22 +117,9 @@
     for load in loads:
         load.start()
 
-    n_a = nx // 2
-    n_b = 2 * ny
     gx = lax.axis_index("gx")
     gy = lax.axis_index("gy")
-    core = lax.rem(gx, 2)
-    col = lax.div(gx, 2)
-    slot_a = col
-    slot_b = core * ny + gy
-
-    def peer_a(step):
-        other = lax.rem(col + step, n_a)
-        return other, (other * 2 + core, gy)
-
-    def peer_b(step):
-        other = lax.rem(slot_b + step, n_b)
-        return other, (col * 2 + lax.div(other, ny), lax.rem(other, ny))
+    groups = [Group(names, nx, ny, gx, gy) for names in STAGES]
 
     exists = {}
     for a, b in BLOCKS:
@@ -108,11 +131,12 @@
         exists[a, b] = inside[0] if len(inside) == 1 else jnp.logical_and(*inside)
 
     barrier = pltpu.get_barrier_semaphore()
-    for step in range(1, n_b):
-        pl.semaphore_signal(barrier, inc=1, device_id=peer_b(step)[1], device_id_type=MESH)
-    for step in range(1, n_a):
-        pl.semaphore_signal(barrier, inc=1, device_id=peer_a(step)[1], device_id_type=MESH)
-    expected = n_a + n_b - 2
+    expected = 0
+    for group in groups:
+        for step in range(1, group.count):
+            pl.semaphore_signal(
+                barrier, inc=1, device_id=group.peer(step)[1], device_id_type=MESH)
+        expected = expected + group.count - 1
     for block in BLOCKS:
         @pl.when(exists[block])
         def _(block=block):
@@ -267,7 +291,7 @@
         v = jnp.broadcast_to(jnp.sum(v, axis=0, keepdims=True), (8, 128))
         return (v + pltpu.roll(v, 32, 1)) + (pltpu.roll(v, 64, 1) + pltpu.roll(v, 96, 1))
 
-    def potentials(turn):
+    def potentials(turn, beside_step):
         depth, start = ROUNDS[turn], STARTS[turn]
         carried = ROUNDS[turn + 1] - 1 if turn + 1 < len(ROUNDS) else 0
         own = (0, 0)
@@ -341,12 +365,13 @@
             planes[start + m, 0:8] = after[own_block][0]
             planes[start + m, 8:16] = after[own_block][1]
             before, now = now, after
+            beside_step(start + m)
         if turn + 1 < len(ROUNDS):
             fill_outbox(turn + 1, *now[own_block], [])
 
     own_block = (0, 0)
 
-    def bulk_shells(k):
+    def bulk_shells(k, unrolled=False):
         scale = (1.0 if is_first(k) else 2.0) / HALF
         current = exchange * (planes[k, 0:8] - planes[k, 8:16])
         center_coef = scale * (1.0 - CENTER + 2.0 * diffusion)
@@ -354,7 +379,7 @@
 
         def shells(base, accs, last):
             accs = list(accs)
-            low = vecs[k, jnp.maximum(base - 1, 0)]
+            low = vecs[k, max(base - 1, 0) if isinstance(base, int) else jnp.maximum(base - 1, 0)]
             here = vecs[k, base]
             for i in range(8):
                 r = base + i
@@ -372,8 +397,12 @@
                 low, here = here, high
             return tuple(accs)
 
-        accs = lax.fori_loop(
-            0, 7, lambda b, accs: shells(b * 8, accs, False), (zero,) * (k + 2))
+        accs = (zero,) * (k + 2)
+        if unrolled:
+            for b in range(7):
+                accs = shells(b * 8, accs, False)
+        else:
+            accs = lax.fori_loop(0, 7, lambda b, accs: shells(b * 8, accs, False), accs)
         return shells(SHELLS - 8, accs, True)
 
     def products(k, accs):
@@ -384,46 +413,42 @@
             keep(k + 1, m, acc)
 
     for turn, start in enumerate(STARTS):
-        accs = bulk_shells(start)
+        end = start + ROUNDS[turn]
+        accs = {start: bulk_shells(start)}
         each_message(turn, functools.partial(receive, turn))
-        potentials(turn)
         if turn + 1 < len(ROUNDS):
+            potentials(turn, lambda k: None)
             send_round(turn + 1)
-        products(start, accs)
-        for k in range(start + 1, start + ROUNDS[turn]):
-            products(k, bulk_shells(k))
-
-    def total(mine, count, slot, peer, sums, s_sem, r_sem):
-        sums[pl.ds(slot, 1)] = mine.reshape(1, 1, 128)
-
-        def copy(step):
-            other, device = peer(step)
-            return other, pltpu.make_async_remote_copy(
-                src_ref=sums.at[slot],
-                dst_ref=sums.at[slot],
-                send_sem=s_sem.at[step],
-                recv_sem=r_sem.at[slot],
-                device_id=device,
-                device_id_type=MESH,
-            )
-
-        for step in range(1, count):
-            copy(step)[1].start()
-        for step in range(1, count):
-            other = peer(step)[0]
-            pltpu.make_async_remote_copy(
-                src_ref=sums.at[other],
-                dst_ref=sums.at[other],
-                send_sem=s_sem.at[step],
-                recv_sem=r_sem.at[other],
-                device_id=peer(step)[1],
-                device_id_type=MESH,
-            ).wait_recv()
-        return jnp.sum(sums[...], axis=0), copy
-
-    mine = jnp.sum(rows[...].T, axis=0, keepdims=True)
-    part, copy_a = total(mine, n_a, slot_a, peer_a, sums_a, as_sem, ar_sem)
-    whole, copy_b = total(part, n_b, slot_b, peer_b, sums_b, bs_sem, br_sem)
+            for k in range(start + 1, end):
+                accs[k] = bulk_shells(k)
+        else:
+            def beside(k):
+                if k < end:
+                    accs[k] = bulk_shells(k, True)
+
+            potentials(turn, beside)
+        for k in range(start, end):
+            products(k, accs[k])
+
+    def copy(stage, slot, step):
+        group = groups[stage]
+        return pltpu.make_async_remote_copy(
+            src_ref=sums[stage].at[slot],
+            dst_ref=sums[stage].at[slot],
+            send_sem=sum_sems[2 * stage].at[step],
+            recv_sem=sum_sems[2 * stage + 1].at[slot],
+            device_id=group.peer(step)[1],
+            device_id_type=MESH,
+        )
+
+    whole = jnp.sum(rows[...].T, axis=0, keepdims=True)
+    for stage, group in enumerate(groups):
+        sums[stage][pl.ds(group.slot, 1)] = whole.reshape(1, 1, 128)
+        for step in range(1, group.count):
+            copy(stage, group.slot, step).start()
+        for step in range(1, group.count):
+            copy(stage, group.peer(step)[0], step).wait_recv()
+        whole = jnp.sum(sums[stage][...], axis=0)
 
     lane2 = lax.broadcasted_iota(jnp.int32, (16, 128), 1)
     sub2 = lax.broadcasted_iota(jnp.int32, (16, 128), 0)
@@ -530,10 +555,9 @@
 
     for turn in range(len(ROUNDS)):
         each_message(turn, lambda block: halo_copy(turn, block).wait_send())
-    for step in range(1, n_a):
-        copy_a(step)[1].wait_send()
-    for step in range(1, n_b):
-        copy_b(step)[1].wait_send()
+    for stage, group in enumerate(groups):
+        for step in range(1, group.count):
+            copy(stage, group.slot, step).wait_send()
 
 
 def results(tall, planes, out_c, out_p):
@@ -550,7 +574,7 @@
 
 
 def fast(nx, ny, *args):
-    n_a, n_b = nx // 2, 2 * ny
+    counts = [members(names, nx, ny) for names in STAGES]
     f32 = jnp.float32
     vmem = pl.BlockSpec(memory_space=pltpu.VMEM)
     tall, planes, flag = pl.pallas_call(
@@ -569,16 +593,12 @@
             pltpu.VMEM((len(ROUNDS), 3, OUTBOX, 128), f32),
             pltpu.VMEM((len(ROUNDS), len(BLOCKS), OUTBOX, 128), f32),
             pltpu.VMEM((128, 128), f32),
-            pltpu.VMEM((n_a, 1, 128), f32),
-            pltpu.VMEM((n_b, 1, 128), f32),
+            *(pltpu.VMEM(a.shape, f32) for a in args),
             pltpu.SemaphoreType.DMA((len(ROUNDS), len(BLOCKS))),
             pltpu.SemaphoreType.DMA((len(ROUNDS), len(BLOCKS))),
-            pltpu.SemaphoreType.DMA((n_a,)),
-            pltpu.SemaphoreType.DMA((n_a,)),
-            pltpu.SemaphoreType.DMA((n_b,)),
-            pltpu.SemaphoreType.DMA((n_b,)),
-            *(pltpu.VMEM(a.shape, f32) for a in args),
             pltpu.SemaphoreType.DMA((5,)),
+            *(pltpu.VMEM((count, 1, 128), f32) for count in counts),
+            *(pltpu.SemaphoreType.DMA((count,)) for count in counts for _ in range(2)),
         ],
         compiler_params=pltpu.CompilerParams(collective_id=0, has_side_effects=True),
     )(*args)

time: 39.2 us -> 37.4 us (0.954)
  Pallas kernels: 37.6 us -> 35.8 us
    pallas_call x1, Pallas kernels: 36.7 us -> 34.9 us  [fast(): pl.pallas_call(functools.partial(kernel, nx, ny), out_shape=(pltpu.VMEM((...]
where the time goes in v4:
time: 37.4 us; the launch traced here: 37.3 us
  Pallas kernels  35.8 us (96%)
  between operations  0.8 us (2%)
  loops' own time  0.75 us (2%)
    pallas_call x1, Pallas kernels, fast(): pl.pallas_call(functools.partial(kernel, nx, ny), out_shape=(pltpu.VMEM((...  34.9 us
    pallas_call x1, Pallas kernels, fast(): pl.pallas_call(results, out_shape=tuple((jax.ShapeDtypeStruct(a.shape, f3...  0.86 us

profile of v4, /device:TPU:1, one launch (start us, length us, event | category | flops | bytes accessed | tf_op | source)
XLA Modules:
  0.0 37.3 jit_solution(16110647846795564221)
XLA Ops:
  0.6 34.9 %shard_map.68 = (f32[512,128]{1,0:T(8,128)S(1)}, f32[16,128]{1,0:T(8,128)S(1)}, f32[1,1]{1,0:T(1,128)}) custom-call(f32[2,16,2048]{2,1,0:T(8,128)} %conc_in.1, f32[2,16,33]{2,1,0:T(8,128)} %pots_in.1, f32[2,16,32]{2,1,0:T(8,128)} %diff_in.1, f32[2,16,32]{2,1,0:T(8,128)} %exch_in.1, f32[2,16,32]{2,1,0:T(8,128)} %slope_in.1), custom_call_target="tpu_custom_call" | custom-call | tf_op jit(solution)/shard_map/pallas_call | solution.py:580
  35.5 0.9 %shard_map.69 = (f32[2,16,2048]{2,1,0:T(8,128)}, f32[2,16,33]{2,1,0:T(8,128)}) custom-call(f32[512,128]{1,0:T(8,128)S(1)} %get-tuple-element.459.tall, f32[16,128]{1,0:T(8,128)S(1)} %get-tuple-element.460.planes), custom_call_target="tpu_custom_call" | custom-call | tf_op jit(solution)/shard_map/pallas_call | solution.py:605
  36.4 0.7 %while.61 = (f32[2,16,2048]{2,1,0:T(8,128)}, f32[2,16,33]{2,1,0:T(8,128)}, f32[]{:T(128)}, f32[2,16,2048]{2,1,0:T(8,128)}, f32[2,16,33]{2,1,0:T(8,128)}, /*index...) while((f32[2,16,2048]{2,1,0:T(8,128)}, f32[2,16,33]{2,1,0:T(8,128)}, f32[]{:T(128)}, ...), condition=%region_22.23_spmd, body=%region_0.22_spmd | while | flops 5886719 | bytes 25668336 | solution.py:743

commit v5 on v4

--- a/solution.py
+++ b/solution.py
@@ -53,6 +53,8 @@
     return 16 + (COEFS if turn == 0 else 0) + 8 * updates
 
 
+MIDDLE = 3
+assert max(abs(a) for a, _ in BLOCKS) <= MIDDLE
 WIDE = 5
 assert DEEPEST <= WIDE
 
@@ -66,40 +68,31 @@
     return names
 
 
-STAGES = (("core",), ("z",), ("x", "y"))
-
-
-def extents(nx, ny):
-    columns = min(4, nx // 2)
-    return {"x": nx // 2 // columns, "y": columns, "core": 2, "z": ny}
-
-
-def members(names, nx, ny):
-    count = 1
-    for name in names:
-        count *= extents(nx, ny)[name]
-    return count
+STAGES = ("core", "z", "plane")
+
+
+def members(name, nx, ny):
+    return {"core": 2, "z": ny, "plane": nx // 2}[name]
 
 
 class Group:
-    def __init__(self, names, nx, ny, gx, gy):
-        self.names, self.extents = names, extents(nx, ny)
-        columns = self.extents["y"]
-        self.place = {"core": lax.rem(gx, 2), "y": lax.rem(lax.div(gx, 2), columns),
-                      "x": lax.div(gx, 2 * columns), "z": gy}
-        self.count = members(names, nx, ny)
-        self.slot = 0
-        for name in names:
-            self.slot = self.slot * self.extents[name] + self.place[name]
+    def __init__(self, name, nx, ny, gx, gy):
+        self.name, self.gx, self.gy = name, gx, gy
+        self.core, self.plane = lax.rem(gx, 2), lax.div(gx, 2)
+        self.count = members(name, nx, ny)
+        self.slot = {"core": self.core, "z": gy, "plane": self.plane}[name]
 
     def peer(self, step):
-        other = lax.rem(self.slot + step, self.count)
-        place, left = dict(self.place), other
-        for name in reversed(self.names):
-            place[name] = lax.rem(left, self.extents[name])
-            left = lax.div(left, self.extents[name])
-        row = (place["x"] * self.extents["y"] + place["y"]) * 2 + place["core"]
-        return other, (row, place["z"])
+        if self.count == 2:
+            other = 1 - self.slot
+        else:
+            other = self.slot + step
+            other = jnp.where(other >= self.count, other - self.count, other)
+        if self.name == "core":
+            return 2 * self.plane + other, self.gy
+        if self.name == "z":
+            return self.gx, other
+        return 2 * other + self.core, self.gy
 
 
 def is_first(k):
@@ -109,7 +102,7 @@
 def kernel(nx, ny, conc_in, pots_in, diff_in, exch_in, slope_in, tall_out, plane_out, flag,
            tall, vecs, planes, outbox, halo, rows, conc, pots, diff, exch, slope, hs_sem, hr_sem, in_sem,
            *for_sums):
-    sums, sum_sems = for_sums[:len(STAGES)], for_sums[len(STAGES):]
+    *sums, sum_sems = for_sums
     loads = [
         pltpu.make_async_copy(source, target, in_sem.at[i])
         for i, (source, target) in enumerate((
@@ -135,7 +128,7 @@
     for group in groups:
         for step in range(1, group.count):
             pl.semaphore_signal(
-                barrier, inc=1, device_id=group.peer(step)[1], device_id_type=MESH)
+                barrier, inc=1, device_id=group.peer(step), device_id_type=MESH)
         expected = expected + group.count - 1
     for block in BLOCKS:
         @pl.when(exists[block])
@@ -287,64 +280,78 @@
         up = jnp.where(jnp.logical_and(sub == 7, quarter == 3), v, up)
         return 2.0 * v - down - up
 
-    def over_nodes(v):
-        v = jnp.broadcast_to(jnp.sum(v, axis=0, keepdims=True), (8, 128))
+    def over_quarters(v):
         return (v + pltpu.roll(v, 32, 1)) + (pltpu.roll(v, 64, 1) + pltpu.roll(v, 96, 1))
+
+    def placed(block):
+        return sub == block[0] + MIDDLE
+
+    inside = {}
+    for b in (-1, 0, 1):
+        inside[b] = jnp.where(placed((0, b)), 1.0, 0.0) if b == 0 else zero
+        for block in BLOCKS:
+            if block[1] == b:
+                inside[b] = jnp.where(
+                    jnp.logical_and(placed(block), exists[block]), 1.0, inside[b])
 
     def potentials(turn, beside_step):
         depth, start = ROUNDS[turn], STARTS[turn]
         carried = ROUNDS[turn + 1] - 1 if turn + 1 < len(ROUNDS) else 0
         own = (0, 0)
-        now = {own: (planes[start, 0:8], planes[start, 8:16],
+        now = {own: (planes[start, 0:8],
                      [vecs[start, SHELLS - 1 - i] for i in range(depth + carried)])}
         coefs = {own: (exchange, slopes, diffusion)}
+        fields = {-1: zero, 0: jnp.where(placed(own), planes[start, 8:16], 0.0), 1: zero}
         for block in BLOCKS:
             if message_rows(turn, block) == 0:
                 continue
             updates = depth - steps_away(block)
             inbox = halo.at[turn, SLOT[block]]
-            if block[1]:
-                side = -block[1]
+            a, b = block
+            if b:
                 names = fields_of(turn, updates)
                 found = {name: inbox[8 * i:8 * i + 8] for i, name in enumerate(names)}
-                shells = [unpack(found["pots"], 2, side)] if updates else []
-                shells += [unpack(found["shells"], i, side) for i in range(updates - 1)]
-                now[block] = (unpack(found["pots"], 0, side), unpack(found["pots"], 1, side), shells)
+                fields[b] = jnp.where(placed(block), found["pots"], fields[b])
+                shells = [unpack(found["pots"], 2, -b)] if updates else []
+                shells += [unpack(found["shells"], i, -b) for i in range(updates - 1)]
+                now[block] = (unpack(found["pots"], 0, -b), shells)
                 if updates:
                     source = halo[0, SLOT[block], 8:16]
-                    coefs[block] = tuple(unpack(source, i, side) for i in range(3))
+                    coefs[block] = tuple(unpack(source, i, -b) for i in range(3))
                 continue
             shells_at = 16 + (COEFS if turn == 0 else 0)
-            now[block] = (inbox[0:8], inbox[8:16],
+            fields[0] = jnp.where(placed(block), inbox[8:16], fields[0])
+            now[block] = (inbox[0:8],
                           [inbox[shells_at + 8 * i:shells_at + 8 * i + 8] for i in range(updates)])
             if updates:
                 source = halo.at[0, SLOT[block]]
                 coefs[block] = (source[16:24], source[24:32], source[32:40])
-        before = None
+        for b in (-1, 1):
+            fields[b] = unpack(fields[b], 1, -b)
+        before = fields_before = None
         for m in range(1, depth + 1):
             scale = (1.0 if m == 1 else 2.0) / HALF
-            after = {}
+            after, fields_after = {}, {}
+            means = {-1: zero, 0: zero, 1: zero}
             for block in now:
                 if steps_away(block) > depth - m:
                     continue
                 a, b = block
-                pot, collector, shells = now[block]
+                pot, shells = now[block]
                 exchange_of, slope_of, diffusion_of = coefs[block]
                 beside = [now.get(other) for other in (
                     (a - 1, b), (a + 1, b), (a, b - 1), (a, b + 1))]
-
-                def lateral(which, own):
-                    return 4.0 * own - around(
-                        own, *(None if other is None else other[which] for other in beside))
-
+                collector = jnp.broadcast_to(fields[b][a + MIDDLE:a + MIDDLE + 1], (8, 128))
                 current = exchange_of * (pot - collector)
+                means[b] = jnp.where(
+                    placed(block),
+                    jnp.broadcast_to(jnp.sum(current, axis=0, keepdims=True), (8, 128)), means[b])
+                lateral = 4.0 * pot - around(
+                    pot, *(None if other is None else other[0] for other in beside))
                 new_pot = scale * (
                     node_cond * node_mirror(pot) + current - slope_of * shells[0]
-                    + plane_cond * lateral(0, pot) - CENTER * pot)
-                new_collector = scale * (
-                    collector_cond * lateral(1, collector)
-                    - over_nodes(current) * (1.0 / 32.0) - CENTER * collector)
-                count = depth - m + carried if block == own_block else depth - steps_away(block) - m
+                    + plane_cond * lateral - CENTER * pot)
+                count = depth - m + carried if block == own else depth - steps_away(block) - m
                 center_coef = scale * (1.0 - CENTER + 2.0 * diffusion_of)
                 side_coef = scale * diffusion_of
                 new_shells = []
@@ -353,23 +360,35 @@
                     if i == 0:
                         new = new + scale * current
                     if m > 1:
-                        new = new - before[block][2][i]
+                        new = new - before[block][1][i]
                     new_shells.append(new)
                 if m > 1:
                     new_pot = new_pot - before[block][0]
-                    new_collector = new_collector - before[block][1]
-                if block != own_block:
+                if block != own:
                     new_pot = jnp.where(exists[block], new_pot, 0.0)
-                    new_collector = jnp.where(exists[block], new_collector, 0.0)
-                after[block] = (new_pot, new_collector, new_shells)
-            planes[start + m, 0:8] = after[own_block][0]
-            planes[start + m, 8:16] = after[own_block][1]
+                after[block] = (new_pot, new_shells)
+            for b in (-1, 0, 1):
+                if m + abs(b) > depth:
+                    fields_after[b] = zero
+                    continue
+                field = fields[b]
+                lateral = 4.0 * field - around(
+                    field, pltpu.roll(field, 1, 0), pltpu.roll(field, 7, 0),
+                    fields.get(b - 1), fields.get(b + 1))
+                new = scale * (collector_cond * lateral
+                               - over_quarters(means[b]) * (1.0 / 32.0) - CENTER * field)
+                if m > 1:
+                    new = new - fields_before[b]
+                fields_after[b] = jnp.where(inside[b] > 0.0, new, 0.0)
+            planes[start + m, 0:8] = after[own][0]
+            planes[start + m, 8:16] = jnp.broadcast_to(
+                fields_after[0][MIDDLE:MIDDLE + 1], (8, 128))
             before, now = now, after
+            fields_before, fields = fields, fields_after
             beside_step(start + m)
         if turn + 1 < len(ROUNDS):
-            fill_outbox(turn + 1, *now[own_block], [])
-
-    own_block = (0, 0)
+            fill_outbox(turn + 1, now[own][0], planes[start + depth, 8:16], now[own][1], [])
+
 
     def bulk_shells(k, unrolled=False):
         scale = (1.0 if is_first(k) else 2.0) / HALF
@@ -430,14 +449,26 @@
         for k in range(start, end):
             products(k, accs[k])
 
-    def copy(stage, slot, step):
+    def copy(stage, step):
         group = groups[stage]
         return pltpu.make_async_remote_copy(
-            src_ref=sums[stage].at[slot],
-            dst_ref=sums[stage].at[slot],
-            send_sem=sum_sems[2 * stage].at[step],
-            recv_sem=sum_sems[2 * stage + 1].at[slot],
-            device_id=group.peer(step)[1],
+            src_ref=sums[stage].at[group.slot],
+            dst_ref=sums[stage].at[group.slot],
+            send_sem=sum_sems.at[stage, 0],
+            recv_sem=sum_sems.at[stage, 1],
+            device_id=group.peer(step),
+            device_id_type=MESH,
+        )
+
+    def all_copies(stage):
+        group = groups[stage]
+        rest = sums[stage].at[pl.ds(0, group.count - 1)]
+        return pltpu.make_async_remote_copy(
+            src_ref=rest,
+            dst_ref=rest,
+            send_sem=sum_sems.at[stage, 0],
+            recv_sem=sum_sems.at[stage, 1],
+            device_id=group.peer(1),
             device_id_type=MESH,
         )
 
@@ -445,9 +476,8 @@
     for stage, group in enumerate(groups):
         sums[stage][pl.ds(group.slot, 1)] = whole.reshape(1, 1, 128)
         for step in range(1, group.count):
-            copy(stage, group.slot, step).start()
-        for step in range(1, group.count):
-            copy(stage, group.peer(step)[0], step).wait_recv()
+            copy(stage, step).start()
+        all_copies(stage).wait_recv()
         whole = jnp.sum(sums[stage][...], axis=0)
 
     lane2 = lax.broadcasted_iota(jnp.int32, (16, 128), 1)
@@ -555,9 +585,8 @@
 
     for turn in range(len(ROUNDS)):
         each_message(turn, lambda block: halo_copy(turn, block).wait_send())
-    for stage, group in enumerate(groups):
-        for step in range(1, group.count):
-            copy(stage, group.slot, step).wait_send()
+    for stage in range(len(STAGES)):
+        all_copies(stage).wait_send()
 
 
 def results(tall, planes, out_c, out_p):
@@ -598,7 +627,7 @@
             pltpu.SemaphoreType.DMA((len(ROUNDS), len(BLOCKS))),
             pltpu.SemaphoreType.DMA((5,)),
             *(pltpu.VMEM((count, 1, 128), f32) for count in counts),
-            *(pltpu.SemaphoreType.DMA((count,)) for count in counts for _ in range(2)),
+            pltpu.SemaphoreType.DMA((len(STAGES), 2)),
         ],
         compiler_params=pltpu.CompilerParams(collective_id=0, has_side_effects=True),
     )(*args)

time: 37.4 us -> 36.6 us (0.979)
  Pallas kernels: 35.8 us -> 35 us
    pallas_call x1, Pallas kernels: 34.9 us -> 34.1 us  [fast(): pl.pallas_call(functools.partial(kernel, nx, ny), out_shape=(pltpu.VMEM((...]
where the time goes in v5:
time: 36.6 us; the launch traced here: 36.5 us
  Pallas kernels  35 us (96%)
  between operations  0.8 us (2%)
  loops' own time  0.75 us (2%)
    pallas_call x1, Pallas kernels, fast(): pl.pallas_call(functools.partial(kernel, nx, ny), out_shape=(pltpu.VMEM((...  34.1 us
    pallas_call x1, Pallas kernels, fast(): pl.pallas_call(results, out_shape=tuple((jax.ShapeDtypeStruct(a.shape, f3...  0.86 us
    another operation x1, loops' own time, shards(): lax.while_loop(lambda state: state[2] < 0.5, again, (conc, pots, flag[0,...  0.75 us

profile of v5, /device:TPU:1, one launch (start us, length us, event | category | flops | bytes accessed | tf_op | source)
XLA Modules:
  0.0 36.5 jit_solution(10237676134137521488)
XLA Ops:
  0.6 34.1 %shard_map.68 = (f32[512,128]{1,0:T(8,128)S(1)}, f32[16,128]{1,0:T(8,128)S(1)}, f32[1,1]{1,0:T(1,128)}) custom-call(f32[2,16,2048]{2,1,0:T(8,128)} %conc_in.1, f32[2,16,33]{2,1,0:T(8,128)} %pots_in.1, f32[2,16,32]{2,1,0:T(8,128)} %diff_in.1, f32[2,16,32]{2,1,0:T(8,128)} %exch_in.1, f32[2,16,32]{2,1,0:T(8,128)} %slope_in.1), custom_call_target="tpu_custom_call" | custom-call | tf_op jit(solution)/shard_map/pallas_call | solution.py:609
  34.7 0.9 %shard_map.69 = (f32[2,16,2048]{2,1,0:T(8,128)}, f32[2,16,33]{2,1,0:T(8,128)}) custom-call(f32[512,128]{1,0:T(8,128)S(1)} %get-tuple-element.459.tall, f32[16,128]{1,0:T(8,128)S(1)} %get-tuple-element.460.planes), custom_call_target="tpu_custom_call" | custom-call | tf_op jit(solution)/shard_map/pallas_call | solution.py:634
  35.6 0.7 %while.61 = (f32[2,16,2048]{2,1,0:T(8,128)}, f32[2,16,33]{2,1,0:T(8,128)}, f32[]{:T(128)}, f32[2,16,2048]{2,1,0:T(8,128)}, f32[2,16,33]{2,1,0:T(8,128)}, /*index...) while((f32[2,16,2048]{2,1,0:T(8,128)}, f32[2,16,33]{2,1,0:T(8,128)}, f32[]{:T(128)}, ...), condition=%region_22.23_spmd, body=%region_0.22_spmd | while | flops 5886719 | bytes 25668336 | solution.py:772

commit v6 on v5

--- a/solution.py
+++ b/solution.py
@@ -99,7 +99,7 @@
     return k in STARTS
 
 
-def kernel(nx, ny, conc_in, pots_in, diff_in, exch_in, slope_in, tall_out, plane_out, flag,
+def kernel(nx, ny, conc_in, pots_in, diff_in, exch_in, slope_in, tall_out, plane_out,
            tall, vecs, planes, outbox, halo, rows, conc, pots, diff, exch, slope, hs_sem, hr_sem, in_sem,
            *for_sums):
     *sums, sum_sems = for_sums
@@ -500,52 +500,54 @@
     diagonal = jnp.broadcast_to(
         jnp.sum(jnp.where(eye, gram, 0.0), axis=1, keepdims=True), (16, 128))
     lengths = jnp.sqrt(jnp.maximum(diagonal, 0.0))
-    beta = jnp.sqrt(jnp.broadcast_to(diagonal[0:1], (16, 128)) + epsilon)
-    inverse = 1.0 / beta
+    start_square = jnp.broadcast_to(diagonal[0:1], (16, 128)) + epsilon
+    inverse = lax.rsqrt(start_square)
+    beta = start_square * inverse
     up_coef = jnp.zeros((16, 128), jnp.float32)
     down_coef = jnp.zeros((16, 128), jnp.float32)
     for k in range(ITERS):
         up_coef = jnp.where(sub2 == k + 1, HALF if is_first(k) else HALF / 2, up_coef)
         if not is_first(k):
             down_coef = jnp.where(sub2 == k - 1, HALF / 2, down_coef)
-    g_lane = jnp.broadcast_to(gram[0:1], (16, 128)) * inverse
-    c_lane = jnp.where(lane2 == 0, inverse, 0.0)
-    g_sub = turned(g_lane)
-    c_sub = jnp.where(sub2 == 0, inverse, 0.0)
-    rest_t = jnp.where(eye, 1.0, 0.0) - g_sub * c_lane
-    gram_rest_t = gram - g_sub * g_lane
-    images = jnp.where(lane2 == 0, g_sub, 0.0)
-    coords = [c_sub]
+
+    u_lane = jnp.where(lane2 == 0, 1.0, 0.0)
+    u_sub = jnp.where(sub2 == 0, 1.0, 0.0)
+    gu_lane = jnp.broadcast_to(gram[0:1], (16, 128))
+    gu_sub = turned(gu_lane)
+    rest_t = jnp.where(eye, 1.0, 0.0)
+    gram_rest_t = gram
+    images = jnp.zeros((16, 128), jnp.float32)
+    coords = []
     trust = jnp.ones((16, 128), jnp.float32)
 
     cosines, sines, inverse_radii, upper = [], [], [], []
     target = [beta[0:1]]
     for j in range(ITERS):
-        w_sub = (CENTER * c_sub + up_coef * pltpu.roll(c_sub, 1, 0)
-                 + down_coef * pltpu.roll(c_sub, 15, 0))
-        u_lane = down(rest_t * w_sub)
-        gu_lane = down(gram_rest_t * w_sub)
-        h_lane = down(images * w_sub)
-        u_sub, gu_sub, h_sub = turned(u_lane), turned(gu_lane), turned(h_lane)
+        image = (CENTER * u_sub + up_coef * pltpu.roll(u_sub, 1, 0)
+                 + down_coef * pltpu.roll(u_sub, 15, 0))
+        p_lane = down(rest_t * image)
+        gp_lane = down(gram_rest_t * image)
+        p_sub, gp_sub = turned(p_lane), turned(gp_lane)
+        h_sub = turned(down(images * image)) * inverse
+        own = down(gu_sub * image) * (inverse * inverse)
+        coords.append(u_sub * inverse)
+        c_lane, g_sub, g_lane = u_lane * inverse, gu_sub * inverse, gu_lane * inverse
+        rest_t = rest_t - g_sub * c_lane
+        gram_rest_t = gram_rest_t - g_sub * g_lane
+        images = jnp.where(lane2 == j, g_sub, images)
+        u_sub, u_lane = (p_sub - u_sub * own) * inverse, (p_lane - u_lane * own) * inverse
+        gu_sub, gu_lane = (gp_sub - gu_sub * own) * inverse, (gp_lane - gu_lane * own) * inverse
         square = down(u_sub * gu_sub)
         spread_square = down(jnp.abs(u_sub) * lengths)
         trust = jnp.where(square > TRUST * spread_square * spread_square, trust, 0.0)
-        height = jnp.sqrt(jnp.maximum(square, 0.0) + epsilon)
-        inverse = 1.0 / height
-        if j + 1 < ITERS:
-            c_sub, g_sub = u_sub * inverse, gu_sub * inverse
-            c_lane, g_lane = u_lane * inverse, gu_lane * inverse
-            rest_t = rest_t - g_sub * c_lane
-            gram_rest_t = gram_rest_t - g_sub * g_lane
-            images = jnp.where(lane2 == j + 1, g_sub, images)
-            coords.append(c_sub)
-        entries = [h_sub[i:i + 1] for i in range(j + 1)] + [height[0:1]]
+        square = jnp.maximum(square, 0.0) + epsilon
+        inverse = lax.rsqrt(square)
+        entries = ([h_sub[i:i + 1] for i in range(j)] + [own[0:1], (square * inverse)[0:1]])
         for row in range(j):
             entries[row], entries[row + 1] = (
                 cosines[row] * entries[row] + sines[row] * entries[row + 1],
                 cosines[row] * entries[row + 1] - sines[row] * entries[row])
-        radius = jnp.sqrt(entries[j] * entries[j] + entries[j + 1] * entries[j + 1])
-        inverse_radius = 1.0 / radius
+        inverse_radius = lax.rsqrt(entries[j] * entries[j] + entries[j + 1] * entries[j + 1])
         cosines.append(entries[j] * inverse_radius)
         sines.append(entries[j + 1] * inverse_radius)
         inverse_radii.append(inverse_radius)
@@ -562,7 +564,7 @@
     coef = weights[0] * coords[0]
     for j in range(1, ITERS):
         coef = coef + weights[j] * coords[j]
-    flag[0, 0] = jnp.min(trust)
+    plane_out[16:24] = trust[0:8]
     coefs = [jnp.broadcast_to(coef[k:k + 1], (8, 128)) for k in range(ITERS)]
 
     def combine(b, carry):
@@ -589,12 +591,13 @@
         all_copies(stage).wait_send()
 
 
-def results(tall, planes, out_c, out_p):
+def results(tall, planes, out_c, out_p, flag):
     for g in range(4):
         block = tall[g * 128:(g + 1) * 128, :].T
         for q in range(4):
             at = (4 * q + g) * 128
             out_c[:, :, at:at + 128] = block[q * 32:(q + 1) * 32].reshape(2, 16, 128)
+    flag[0, 0] = jnp.min(planes[16:24])
     sol = planes[0:8]
     by_node = [sol if q == 0 else pltpu.roll(sol, 128 - 32 * q, 1) for q in range(4)]
     by_node = jnp.concatenate(
@@ -606,15 +609,14 @@
     counts = [members(names, nx, ny) for names in STAGES]
     f32 = jnp.float32
     vmem = pl.BlockSpec(memory_space=pltpu.VMEM)
-    tall, planes, flag = pl.pallas_call(
+    tall, planes = pl.pallas_call(
         functools.partial(kernel, nx, ny),
         out_shape=(
             pltpu.VMEM((512, 128), f32),
-            pltpu.VMEM((16, 128), f32),
-            jax.ShapeDtypeStruct((1, 1), f32),
+            pltpu.VMEM((24, 128), f32),
         ),
         in_specs=[pl.BlockSpec(memory_space=pltpu.HBM)] * 5,
-        out_specs=(vmem, vmem, pl.BlockSpec(memory_space=pltpu.SMEM)),
+        out_specs=(vmem, vmem),
         scratch_shapes=[
             pltpu.VMEM((512, 128), f32),
             pltpu.VMEM((DIM, SHELLS, 8, 128), f32),
@@ -631,13 +633,13 @@
         ],
         compiler_params=pltpu.CompilerParams(collective_id=0, has_side_effects=True),
     )(*args)
-    conc, pots = pl.pallas_call(
+    return pl.pallas_call(
         results,
-        out_shape=tuple(jax.ShapeDtypeStruct(a.shape, f32) for a in args[:2]),
+        out_shape=(*(jax.ShapeDtypeStruct(a.shape, f32) for a in args[:2]),
+                   jax.ShapeDtypeStruct((1, 1), f32)),
         in_specs=[vmem] * 2,
-        out_specs=(vmem,) * 2,
+        out_specs=(vmem, vmem, pl.BlockSpec(memory_space=pltpu.SMEM)),
     )(*(pltpu.with_memory_space_constraint(a, pltpu.VMEM) for a in (tall, planes)))
-    return conc, pots, flag
 
 
 def with_halo(shard, sides, width):

time: 36.6 us -> 35.7 us (0.975)
  Pallas kernels: 35 us -> 34.1 us
    pallas_call x1, Pallas kernels: 34.1 us -> 33.2 us  [fast(): pl.pallas_call(functools.partial(kernel, nx, ny), out_shape=(pltpu.VMEM((...]
where the time goes in v6:
time: 35.7 us; the launch traced here: 35.6 us
  Pallas kernels  34.1 us (96%)
  between operations  0.81 us (2%)
  loops' own time  0.75 us (2%)
    pallas_call x1, Pallas kernels, fast(): pl.pallas_call(functools.partial(kernel, nx, ny), out_shape=(pltpu.VMEM((...  33.2 us
    pallas_call x1, Pallas kernels, fast(): pl.pallas_call(results, out_shape=(*(jax.ShapeDtypeStruct(a.shape, f32) f...  0.88 us
    another operation x1, loops' own time, shards(): lax.while_loop(lambda state: state[2] < 0.5, again, (conc, pots, flag[0,...  0.75 us

profile of v6, /device:TPU:1, one launch (start us, length us, event | category | flops | bytes accessed | tf_op | source)
XLA Modules:
  0.0 35.6 jit_solution(3308767905794633649)
XLA Ops:
  0.6 33.2 %shard_map.68 = (f32[512,128]{1,0:T(8,128)S(1)}, f32[24,128]{1,0:T(8,128)S(1)}) custom-call(f32[2,16,2048]{2,1,0:T(8,128)} %conc_in.1, f32[2,16,33]{2,1,0:T(8,128)} %pots_in.1, f32[2,16,32]{2,1,0:T(8,128)} %diff_in.1, f32[2,16,32]{2,1,0:T(8,128)} %exch_in.1, f32[2,16,32]{2,1,0:T(8,128)} %slope_in.1), custom_call_target="tpu_custom_call" | custom-call | tf_op jit(solution)/shard_map/pallas_call | solution.py:612
  33.8 0.9 %shard_map.69 = (f32[2,16,2048]{2,1,0:T(8,128)}, f32[2,16,33]{2,1,0:T(8,128)}, f32[1,1]{1,0:T(1,128)}) custom-call(f32[512,128]{1,0:T(8,128)S(1)} %get-tuple-element.459.tall, f32[24,128]{1,0:T(8,128)S(1)} %get-tuple-element.460.planes), custom_call_target="tpu_custom_call" | custom-call | tf_op jit(solution)/shard_map/pallas_call | solution.py:636
  34.7 0.7 %while.61 = (f32[2,16,2048]{2,1,0:T(8,128)}, f32[2,16,33]{2,1,0:T(8,128)}, f32[]{:T(128)}, f32[2,16,2048]{2,1,0:T(8,128)}, f32[2,16,33]{2,1,0:T(8,128)}, /*index...) while((f32[2,16,2048]{2,1,0:T(8,128)}, f32[2,16,33]{2,1,0:T(8,128)}, f32[]{:T(128)}, ...), condition=%region_22.23_spmd, body=%region_0.22_spmd | while | flops 5886719 | bytes 25668336 | solution.py:774

commit v7 on v6

--- a/solution.py
+++ b/solution.py
@@ -19,7 +19,7 @@
 ROUNDS = (5, 5)
 CENTER = 11.0
 HALF = 10.0
-TRUST = 1e-4
+TRUST = 4e-4
 
 CELLS = 32
 SHELLS = 64

time: 35.7 us -> 35.7 us (level)
  no operation moved by 1% of the time
where the time goes in v7:
time: 35.7 us; the launch traced here: 35.6 us
  Pallas kernels  34.1 us (96%)
  between operations  0.81 us (2%)
  loops' own time  0.75 us (2%)
    pallas_call x1, Pallas kernels, fast(): pl.pallas_call(functools.partial(kernel, nx, ny), out_shape=(pltpu.VMEM((...  33.2 us
    pallas_call x1, Pallas kernels, fast(): pl.pallas_call(results, out_shape=(*(jax.ShapeDtypeStruct(a.shape, f32) f...  0.88 us
    another operation x1, loops' own time, shards(): lax.while_loop(lambda state: state[2] < 0.5, again, (conc, pots, flag[0,...  0.75 us

profile of v7, /device:TPU:1, one launch (start us, length us, event | category | flops | bytes accessed | tf_op | source)
XLA Modules:
  0.0 35.6 jit_solution(10682610964575324974)
XLA Ops:
  0.6 33.2 %shard_map.68 = (f32[512,128]{1,0:T(8,128)S(1)}, f32[24,128]{1,0:T(8,128)S(1)}) custom-call(f32[2,16,2048]{2,1,0:T(8,128)} %conc_in.1, f32[2,16,33]{2,1,0:T(8,128)} %pots_in.1, f32[2,16,32]{2,1,0:T(8,128)} %diff_in.1, f32[2,16,32]{2,1,0:T(8,128)} %exch_in.1, f32[2,16,32]{2,1,0:T(8,128)} %slope_in.1), custom_call_target="tpu_custom_call" | custom-call | tf_op jit(solution)/shard_map/pallas_call | solution.py:612
  33.8 0.9 %shard_map.69 = (f32[2,16,2048]{2,1,0:T(8,128)}, f32[2,16,33]{2,1,0:T(8,128)}, f32[1,1]{1,0:T(1,128)}) custom-call(f32[512,128]{1,0:T(8,128)S(1)} %get-tuple-element.459.tall, f32[24,128]{1,0:T(8,128)S(1)} %get-tuple-element.460.planes), custom_call_target="tpu_custom_call" | custom-call | tf_op jit(solution)/shard_map/pallas_call | solution.py:636
  34.7 0.7 %while.61 = (f32[2,16,2048]{2,1,0:T(8,128)}, f32[2,16,33]{2,1,0:T(8,128)}, f32[]{:T(128)}, f32[2,16,2048]{2,1,0:T(8,128)}, f32[2,16,33]{2,1,0:T(8,128)}, /*index...) while((f32[2,16,2048]{2,1,0:T(8,128)}, f32[2,16,33]{2,1,0:T(8,128)}, f32[]{:T(128)}, ...), condition=%region_22.23_spmd, body=%region_0.22_spmd | while | flops 5886719 | bytes 25668336 | solution.py:774

commit v8 on v7

--- a/solution.py
+++ b/solution.py
@@ -442,10 +442,12 @@
                 accs[k] = bulk_shells(k)
         else:
             def beside(k):
+                products(k - 1, accs[k - 1])
                 if k < end:
                     accs[k] = bulk_shells(k, True)
 
             potentials(turn, beside)
+            continue
         for k in range(start, end):
             products(k, accs[k])
 

time: 35.7 us -> 35.7 us (level)
  no operation moved by 1% of the time
where the time goes in v8:
time: 35.7 us; the launch traced here: 35.6 us
  Pallas kernels  34 us (95%)
  between operations  0.81 us (2%)
  loops' own time  0.75 us (2%)
    pallas_call x1, Pallas kernels, fast(): pl.pallas_call(functools.partial(kernel, nx, ny), out_shape=(pltpu.VMEM((...  33.2 us
    pallas_call x1, Pallas kernels, fast(): pl.pallas_call(results, out_shape=(*(jax.ShapeDtypeStruct(a.shape, f32) f...  0.88 us
    another operation x1, loops' own time, shards(): lax.while_loop(lambda state: state[2] < 0.5, again, (conc, pots, flag[0,...  0.75 us

profile of v8, /device:TPU:1, one launch (start us, length us, event | category | flops | bytes accessed | tf_op | source)
XLA Modules:
  0.0 35.6 jit_solution(1894264637975454066)
XLA Ops:
  0.6 33.2 %shard_map.68 = (f32[512,128]{1,0:T(8,128)S(1)}, f32[24,128]{1,0:T(8,128)S(1)}) custom-call(f32[2,16,2048]{2,1,0:T(8,128)} %conc_in.1, f32[2,16,33]{2,1,0:T(8,128)} %pots_in.1, f32[2,16,32]{2,1,0:T(8,128)} %diff_in.1, f32[2,16,32]{2,1,0:T(8,128)} %exch_in.1, f32[2,16,32]{2,1,0:T(8,128)} %slope_in.1), custom_call_target="tpu_custom_call" | custom-call | tf_op jit(solution)/shard_map/pallas_call | solution.py:614
  33.8 0.9 %shard_map.69 = (f32[2,16,2048]{2,1,0:T(8,128)}, f32[2,16,33]{2,1,0:T(8,128)}, f32[1,1]{1,0:T(1,128)}) custom-call(f32[512,128]{1,0:T(8,128)S(1)} %get-tuple-element.459.tall, f32[24,128]{1,0:T(8,128)S(1)} %get-tuple-element.460.planes), custom_call_target="tpu_custom_call" | custom-call | tf_op jit(solution)/shard_map/pallas_call | solution.py:638
  34.7 0.7 %while.61 = (f32[2,16,2048]{2,1,0:T(8,128)}, f32[2,16,33]{2,1,0:T(8,128)}, f32[]{:T(128)}, f32[2,16,2048]{2,1,0:T(8,128)}, f32[2,16,33]{2,1,0:T(8,128)}, /*index...) while((f32[2,16,2048]{2,1,0:T(8,128)}, f32[2,16,33]{2,1,0:T(8,128)}, f32[]{:T(128)}, ...), condition=%region_22.23_spmd, body=%region_0.22_spmd | while | flops 5886719 | bytes 25668336 | solution.py:776

commit v9 on v7

--- a/solution.py
+++ b/solution.py
@@ -433,7 +433,7 @@
 
     for turn, start in enumerate(STARTS):
         end = start + ROUNDS[turn]
-        accs = {start: bulk_shells(start)}
+        accs = {start: bulk_shells(start, True)}
         each_message(turn, functools.partial(receive, turn))
         if turn + 1 < len(ROUNDS):
             potentials(turn, lambda k: None)

time: 35.7 us -> 35.7 us (level)
  no operation moved by 1% of the time
where the time goes in v9:
time: 35.7 us; the launch traced here: 35.6 us
  Pallas kernels  34.1 us (96%)
  between operations  0.81 us (2%)
  loops' own time  0.75 us (2%)
    pallas_call x1, Pallas kernels, fast(): pl.pallas_call(functools.partial(kernel, nx, ny), out_shape=(pltpu.VMEM((...  33.2 us
    pallas_call x1, Pallas kernels, fast(): pl.pallas_call(results, out_shape=(*(jax.ShapeDtypeStruct(a.shape, f32) f...  0.88 us
    another operation x1, loops' own time, shards(): lax.while_loop(lambda state: state[2] < 0.5, again, (conc, pots, flag[0,...  0.75 us

profile of v9, /device:TPU:1, one launch (start us, length us, event | category | flops | bytes accessed | tf_op | source)
XLA Modules:
  0.0 35.6 jit_solution(6577649936234412790)
XLA Ops:
  0.6 33.2 %shard_map.68 = (f32[512,128]{1,0:T(8,128)S(1)}, f32[24,128]{1,0:T(8,128)S(1)}) custom-call(f32[2,16,2048]{2,1,0:T(8,128)} %conc_in.1, f32[2,16,33]{2,1,0:T(8,128)} %pots_in.1, f32[2,16,32]{2,1,0:T(8,128)} %diff_in.1, f32[2,16,32]{2,1,0:T(8,128)} %exch_in.1, f32[2,16,32]{2,1,0:T(8,128)} %slope_in.1), custom_call_target="tpu_custom_call" | custom-call | tf_op jit(solution)/shard_map/pallas_call | solution.py:612
  33.8 0.9 %shard_map.69 = (f32[2,16,2048]{2,1,0:T(8,128)}, f32[2,16,33]{2,1,0:T(8,128)}, f32[1,1]{1,0:T(1,128)}) custom-call(f32[512,128]{1,0:T(8,128)S(1)} %get-tuple-element.459.tall, f32[24,128]{1,0:T(8,128)S(1)} %get-tuple-element.460.planes), custom_call_target="tpu_custom_call" | custom-call | tf_op jit(solution)/shard_map/pallas_call | solution.py:636
  34.7 0.7 %while.61 = (f32[2,16,2048]{2,1,0:T(8,128)}, f32[2,16,33]{2,1,0:T(8,128)}, f32[]{:T(128)}, f32[2,16,2048]{2,1,0:T(8,128)}, f32[2,16,33]{2,1,0:T(8,128)}, /*index...) while((f32[2,16,2048]{2,1,0:T(8,128)}, f32[2,16,33]{2,1,0:T(8,128)}, f32[]{:T(128)}, ...), condition=%region_22.23_spmd, body=%region_0.22_spmd | while | flops 5886719 | bytes 25668336 | solution.py:774
